TPU v7x, 256 devices: a whole 4x4x8 slice. The times are simulated.
256 devices in a mesh: section: 8 (over y, core), replica: 32 (over z, x).
Axes of the slice: x: 4, y: 4, z: 8, core: 2. Of those that a mesh axis runs over, the one named last changes fastest.
Arguments:
- gradient: bfloat16 [1024, 131072], P('section', 'replica'), may hold values from -1300 to 1300
- residual: float32 [1024, 131072], P('section', 'replica'), may hold values from -6 to 6
- block_ids: int32 [8, 256], P('section', 'replica'), may hold values from 0 to 15, as said below
- block_counts: int32 [8, 32], P('section', 'replica'), may hold values from 1 to 8, as said below
Outputs:
- new_residual: float32 [1024, 131072], P('section', 'replica')
- update: bfloat16 [1024, 4096], P('section', 'replica')
Inputs may be any that keep to these rules, and one draw needn't show every extreme that they name: `block_ids`: each device's 8 block numbers are distinct; only the first block_counts of them are selected. `block_counts`: in every section some replica selects exactly 8 blocks; the others select at most 4.
All inputs are finite; a program needn't handle non-finite values.
Results may differ from a plain program's by a relative error of at most 0.013.
Values may be sent and summed in bfloat16 or wider, within the bound.
A program may use at most 64 MiB of HBM per device.

v0:
```python
import jax
import jax.numpy as jnp
from jax import lax
from jax.sharding import Mesh
from jax.sharding import PartitionSpec as P

BLK = 8
REPLICA = ("replica_0", "replica_1")
SECTION = ("section_0", "section_1")


scale_level = 1.0
epsilon = 1e-06


def gathered_by_axis(x, axes, dim):
    if not axes:
        return x
    nearer = lax.all_gather(x, axes[-1], axis=dim, tiled=True)
    return gathered_by_axis(nearer, axes[:-1], dim)


def sent_to_all(x, axis):
    copies = jnp.broadcast_to(x, (lax.axis_size(axis), *x.shape))
    return lax.all_to_all(copies, axis, split_axis=0, concat_axis=0, tiled=True)


def of_everyone(x, axis):
    return sent_to_all(x, axis).sum(axis=0)


def by_axis(x, axes):
    far, near = axes
    return of_everyone(of_everyone(x, near), far)


def deposit(packed, owners, block_total):
    one_hot = (owners[:, None] == jnp.arange(block_total, dtype=jnp.int32)[None, :]).astype(
        jnp.bfloat16
    )
    return jnp.einsum("kb,kxc->bxc", one_hot, packed, preferred_element_type=jnp.float32)


def per_device(gradient, residual, block_ids, block_counts):
    row_count, width = gradient.shape
    replicas = lax.axis_size(REPLICA)
    col_count = width // replicas
    block_total = row_count // BLK
    slot_count = block_ids.shape[1]
    accumulated = gradient.astype(jnp.float32) + residual
    slot_ids = block_ids[0]
    live_slot = jnp.arange(slot_count, dtype=jnp.int32) < block_counts[0, 0]
    hit_table = (
        slot_ids[:, None] == jnp.arange(block_total, dtype=jnp.int32)[None, :]
    ) & live_slot[:, None]
    chosen = jnp.any(hit_table, axis=0)
    row_chosen = jnp.repeat(chosen, BLK)[:, None]
    sent = jnp.where(
        row_chosen, accumulated.astype(jnp.bfloat16).astype(jnp.float32), jnp.float32(0.0)
    )
    new_residual = accumulated - sent
    picked = accumulated.reshape(block_total, BLK, width)[slot_ids]
    packed_blocks = jnp.where(live_slot[:, None, None], picked, jnp.float32(0.0)).astype(
        jnp.bfloat16
    )
    column_parts = packed_blocks.reshape(slot_count, BLK, replicas, col_count)
    received = lax.all_to_all(column_parts, REPLICA, split_axis=2, concat_axis=0, tiled=True)
    owners = gathered_by_axis(slot_ids, REPLICA, 0)
    flat_received = received.reshape(replicas * slot_count, BLK, col_count)
    summed = deposit(flat_received, owners, block_total).reshape(row_count, col_count)
    local_square = jnp.sum(summed * summed)
    norm_total = by_axis(local_square, ("section_0", ("section_1", "replica_0", "replica_1")))
    element_count = lax.axis_size(SECTION) * row_count * width
    root_mean = jnp.sqrt(norm_total / element_count + epsilon)
    clip_factor = scale_level / root_mean
    update = (summed * clip_factor).astype(jnp.bfloat16)
    return (new_residual, update)


def solution(mesh):
    split = Mesh(
        mesh.devices.reshape(4, 2, 8, 4), ("section_0", "section_1", "replica_0", "replica_1")
    )
    return jax.shard_map(
        per_device,
        mesh=split,
        in_specs=(
            P(SECTION, REPLICA),
            P(SECTION, REPLICA),
            P(SECTION, REPLICA),
            P(SECTION, REPLICA),
        ),
        out_specs=(P(SECTION, REPLICA), P(SECTION, REPLICA)),
        check_vma=False,
    )
```

profile of v0, /device:TPU:1, one launch (start us, length us, event | category | flops | bytes accessed | tf_op | source)
XLA Modules:
  0.0 75.2 jit_solution(2620851719656784843)
XLA Ops:
  1.3 0.7 fusion.10
  2.0 2.1 %fusion.1 = bf16[16,8,4096]{2,1,0:T(8,128)(2,1)S(1)} fusion(f32[128,4096]{1,0:T(8,128)} %param.5, bf16[128,4096]{1,0:T(8,128)(2,1)} %param.4), kind=kLoop, calls=%fused_computation.5 | loop fusion | flops 1572864 | bytes 4194304 | tf_op jit(solution)/shard_map/reshape | solution.py:62
  4.0 0.0 copy-start.4
  4.0 0.0 copy-start.3
  4.1 0.0 copy-start.2
  4.1 1.4 %gather_fusion = bf16[8,8,4096]{2,1,0:T(8,128)(2,1)} fusion(bf16[16,8,4096]{2,1,0:T(8,128)(2,1)S(1)} %fusion.1, s32[1024]{0:T(1024)S(1)} %pad_clamp_fusion), kind=kCustom, calls=%fused_computation | custom fusion | bytes 1048608 | tf_op jit(solution)/shard_map/gather | solution.py:62
  5.4 1.4 %fusion = bf16[8,8,32,128]{3,2,1,0:T(8,128)(2,1)S(1)} fusion(bf16[8,8,32,128]{3,1,2,0:T(8,128)(2,1)} %bitcast.35, pred[8]{0:T(512)(128)(4,1)S(1)} %iota_compare_fusion.2), kind=kLoop, calls=%fused_computation.4 | loop fusion | flops 262144 | bytes 1048584 | tf_op jit(solution)/shard_map/convert_element_type | solution.py:63
  6.8 1.0 %copy.14 = bf16[8,8,32,128]{3,1,0,2:T(8,128)(2,1)} copy(bf16[8,8,32,128]{3,2,1,0:T(8,128)(2,1)S(1)} %fusion) | data formatting | bytes 1048576 | tf_op jit(solution)/shard_map/convert_element_type | solution.py:63
  7.8 12.0 %all-to-all-start = ((bf16[8,8,32,128]{3,1,0,2:T(8,128)(2,1)}), bf16[8,8,32,128]{3,1,0,2:T(8,128)(2,1)}, u32[]{:S(2)}, u32[]{:S(2)}) async-start(bf16[8,8,32,128]{3,1,0,2:T(8,128)(2,1)} %copy.14), calls=%async_computation | async-start | bytes 1048576 | tf_op jit(solution)/shard_map/all_to_all | solution.py:67
  19.8 0.0 copy-done.4
  19.8 0.7 dynamic-slice.1
  20.5 0.0 copy-done.3
  20.5 0.6 dynamic-slice
  21.1 0.0 copy-done.2
  21.1 0.1 fusion.9
  21.2 0.1 broadcast_in_dim.41
  21.2 0.1 broadcast_in_dim.42
  22.7 0.1 bitcast_dynamic-update-slice_fusion
  22.8 8.0 %all-reduce = s32[32]{0:T(128)S(1)} all-reduce(s32[32]{0:T(128)S(1)} %bitcast_dynamic-update-slice_fusion), channel_id=2, replica_groups=mesh['section_0'=4,'section_1'=2,'replica_0'=8,'replica_1'=4] {'replica_1'}, use_global_device_ids=true, to_apply=%add | all-reduce | flops 32 | bytes 256
  30.8 0.2 dynamic-update-slice.1
  31.0 11.0 %all-reduce.1 = s32[256]{0:T(256)S(1)} all-reduce(s32[256]{0:T(256)S(1)} %dynamic-update-slice.1), channel_id=3, replica_groups=mesh['section_0'=4,'section_1'=2,'replica_0'=8,'replica_1'=4] {'replica_0'}, use_global_device_ids=true, to_apply=%add.1 | all-reduce | flops 256 | bytes 2048
  42.0 0.0 all-to-all-done
  42.0 1.8 %multiply_reduce_fusion = (f32[]{:T(128)}, f32[16,8,128]{2,0,1:T(8,128)S(1)}) fusion(bf16[32,8,8,1,128]{4,2,1,0,3:T(8,128)(2,1)} %bitcast.9, s32[256]{0:T(256)S(1)} %all-reduce.1), kind=kOutput, calls=%fused_computation.10 | convolution fusion | flops 8425471 | bytes 590852 | tf_op jit(solution)/shard_map/kb,kxc->bxc/dot_general | solution.py:41
  43.8 1.3 %broadcast_in_dim.47 = f32[64,1,1]{2,1,0:T(1,128)} broadcast(f32[]{:T(128)} %get-tuple-element.2), dimensions={} | broadcast | bytes 260 | tf_op jit(solution)/shard_map/broadcast_in_dim | solution.py:24
  45.1 9.7 %all-to-all-start.1 = ((f32[64,1,1]{2,1,0:T(1,128)}), f32[64,1,1]{2,1,0:T(1,128)S(1)}, u32[]{:S(2)}, u32[]{:S(2)}) async-start(f32[64,1,1]{2,1,0:T(1,128)} %broadcast_in_dim.47), calls=%async_computation.1 | async-start | bytes 65536 | tf_op jit(solution)/shard_map/all_to_all | solution.py:25
  54.8 1.7 %select_subtract_fusion = f32[128,4096]{1,0:T(8,128)} fusion(f32[128,4096]{1,0:T(8,128)S(1)} %copy-done, bf16[128,4096]{1,0:T(8,128)(2,1)S(1)} %copy-done.1, pred[128]{0:T(512)(128)(4,1)S(1)} %broadcast_in_dim.42), kind=kLoop, calls=%fused_computation.1 | loop fusion | flops 3145728 | bytes 5243008 | tf_op jit(solution)/shard_map/sub | solution.py:61
  56.5 7.4 %all-to-all-done.1 = f32[64,1,1]{2,1,0:T(1,128)S(1)} async-done(((f32[64,1,1]{2,1,0:T(1,128)}), f32[64,1,1]{2,1,0:T(1,128)S(1)}, u32[]{:S(2)}, u32[]{:S(2)}) %all-to-all-start.1) | async-done | bytes 288 | tf_op jit(solution)/shard_map/all_to_all | solution.py:25
  63.8 0.7 reduce_sum.28
  64.5 0.6 broadcast_in_dim.48
  65.1 8.1 %all_to_all.27 = f32[4,1,1]{2,1,0:T(1,128)S(1)} all-to-all(f32[4,1,1]{2,1,0:T(1,128)S(1)} %broadcast_in_dim.48), channel_id=1, replica_groups=mesh['section_0'=4,'section_1'=2,'replica_0'=8,'replica_1'=4] {'section_0'}, dimensions={0} | all-to-all | bytes 32 | tf_op jit(solution)/shard_map/all_to_all | solution.py:25
  73.3 0.6 reduce_sum.29
  74.6 0.6 copy.30
  (9 shorter events, 0.0 us)
Async XLA Ops:
  4.0 15.8 %copy-start.4 = (u32[256]{0:T(256)S(1)}, u32[256]{0:T(256)}, u32[]{:S(2)}) copy-start(u32[256]{0:T(256)} %constant.23) | copy-start | bytes 3076
  4.0 16.5 %copy-start.3 = (u32[256]{0:T(256)S(1)}, u32[256]{0:T(256)}, u32[]{:S(2)}) copy-start(u32[256]{0:T(256)} %constant.18) | copy-start | bytes 3076
  4.1 17.0 %copy-start.2 = (s32[1,8]{1,0:T(1,128)S(1)}, s32[1,8]{1,0:T(1,128)}, u32[]{:S(2)}) copy-start(s32[1,8]{1,0:T(1,128)} %param.6) | copy-start | bytes 100
  5.4 49.3 %copy-start = (f32[128,4096]{1,0:T(8,128)S(1)}, f32[128,4096]{1,0:T(8,128)}, u32[]{:S(2)}) copy-start(f32[128,4096]{1,0:T(8,128)} %param.5) | copy-start | bytes 6291460
  5.4 49.3 %copy-start.1 = (bf16[128,4096]{1,0:T(8,128)(2,1)S(1)}, bf16[128,4096]{1,0:T(8,128)(2,1)}, u32[]{:S(2)}) copy-start(bf16[128,4096]{1,0:T(8,128)(2,1)} %param.4) | copy-start | bytes 3145732
  7.8 34.2 %all-to-all-start = ((bf16[8,8,32,128]{3,1,0,2:T(8,128)(2,1)}), bf16[8,8,32,128]{3,1,0,2:T(8,128)(2,1)}, u32[]{:S(2)}, u32[]{:S(2)}) async-start(bf16[8,8,32,128]{3,1,0,2:T(8,128)(2,1)} %copy.14), calls=%async_computation | async-start | bytes 1048576 | tf_op jit(solution)/shard_map/all_to_all | solution.py:67
  45.1 18.7 %all-to-all-start.1 = ((f32[64,1,1]{2,1,0:T(1,128)}), f32[64,1,1]{2,1,0:T(1,128)S(1)}, u32[]{:S(2)}, u32[]{:S(2)}) async-start(f32[64,1,1]{2,1,0:T(1,128)} %broadcast_in_dim.47), calls=%async_computation.1 | async-start | bytes 65536 | tf_op jit(solution)/shard_map/all_to_all | solution.py:25
where the time goes:
time: 75.6 us; the launch traced here: 75.2 us
  blocking collectives  27.1 us (36%)
  starting transfers between devices  21.7 us (29%)
  waiting for transfers between devices  7.37 us (10%)
  other arithmetic  7.14 us (9%)
  local copies, waits for them, and re-layouts  6.66 us (9%)
  between operations  3.44 us (5%)
  matrix products  1.84 us (2%)
    unnamed x2, blocking collectives  19 us
    all_to_all x1, starting transfers between devices, per_device(): lax.all_to_all(column_parts, REPLICA, split_axis=2, concat_axis=0, tiled=...  12 us
    all_to_all x1, starting transfers between devices, sent_to_all(): return lax.all_to_all(copies, axis, split_axis=0, concat_axis=0, tiled=True)  9.67 us
    all_to_all x1, blocking collectives, sent_to_all(): return lax.all_to_all(copies, axis, split_axis=0, concat_axis=0, tiled=True)  8.12 us
    all_to_all x1, waiting for transfers between devices, sent_to_all(): return lax.all_to_all(copies, axis, split_axis=0, concat_axis=0, tiled=True)  7.37 us
    reshape x1, other arithmetic, per_device(): picked = accumulated.reshape(block_total, BLK, width)[slot_ids]  2.06 us
    broadcast_in_dim x2, local copies, waits for them, and re-layouts, sent_to_all(): copies = jnp.broadcast_to(x, (lax.axis_size(axis), *x.shape))  1.92 us
    dot_general x1, matrix products, deposit(): jnp.einsum('kb,kxc->bxc', one_hot, packed, preferred_element_type=jnp.flo...  1.84 us
  transfers between devices with their start and end apart: 2, of which 1 were waited for; matrix products, arithmetic and copies ran while one was open for 5% of the time, Pallas kernels for 0%

commit v1 on v0

v1 whole, which is shorter than its diff:
```python
import functools
import jax
import jax.numpy as jnp
from jax import lax
from jax.experimental import pallas as pl
from jax.experimental.pallas import tpu as pltpu
from jax.sharding import PartitionSpec as P

BLK = 8
LANES = 128
MESH = pl.DeviceIdType.MESH

scale_level = 1.0
epsilon = 1e-06


def plane_order(nz, nx):
    offsets = [(dz, dx) for dz in range(nz) for dx in range(nx) if (dz, dx) != (0, 0)]
    far = lambda d, n: min(d, n - d)
    return sorted(offsets, key=lambda o: (-far(o[0], nz) - far(o[1], nx), far(o[1], nx), o))


def kernel(
    nz, nx, sections, count_total,
    grad_hbm, res_hbm, ids_ref, count_ref,
    new_res, update,
    grad, res, packed, rows_out, recv, rows_in, sums, sums_a, sums_b,
    load_sem, data_send, data_recv, rows_send, rows_recv, a_send, a_recv, b_send, b_recv,
):
    replicas = nz * nx
    blocks, _, width = grad.shape
    row_count = blocks * BLK
    cols = width // replicas
    slots = ids_ref.shape[1]
    sec, rep = lax.axis_index("section"), lax.axis_index("replica")
    z, x = rep // nx, rep % nx

    loads = []
    chunks = 4
    step = blocks // chunks
    for c in range(chunks):
        part = pl.ds(c * step, step)
        pair = (
            pltpu.make_async_copy(grad_hbm.at[part], grad.at[part], load_sem.at[0, c]),
            pltpu.make_async_copy(res_hbm.at[part], res.at[part], load_sem.at[1, c]),
        )
        for copy in pair:
            copy.start()
        loads.append(pair)

    plane = []
    for dz, dx in plane_order(nz, nx):
        plane.append(((z + dz) % nz) * nx + (x + dx) % nx)
    across = [(sec + d) % sections for d in range(1, sections)]
    barrier = pltpu.get_barrier_semaphore()
    for peer in plane:
        pl.semaphore_signal(barrier, inc=1, device_id=(sec, peer), device_id_type=MESH)
    for peer in across:
        pl.semaphore_signal(barrier, inc=1, device_id=(peer, rep), device_id_type=MESH)

    lane = lax.broadcasted_iota(jnp.int32, (1, LANES), 1)
    half = rep % 2
    slot_of = lane // BLK - half * slots
    count = jnp.full((1, LANES), count_ref[0, 0], jnp.int32)
    ids = [jnp.full((1, LANES), ids_ref[0, s], jnp.int32) for s in range(slots)]
    ids = [jnp.where(count > s, ids[s], -1) for s in range(slots)]
    target = jnp.full((1, LANES), -1, jnp.int32)
    for s in range(slots):
        target = jnp.where(slot_of == s, ids[s] * BLK + lane % BLK, target)
    rows_out[0] = target
    rows_in[pl.ds(rep, 1)] = target[None]

    per_chunk = blocks // chunks
    for c in range(chunks):
        for copy in loads[c]:
            copy.wait()
        for b in range(c * per_chunk, (c + 1) * per_chunk):
            mine = grad[b].astype(jnp.float32) + res[b]
            res[b] = mine
            hit = jnp.zeros((1, LANES), jnp.float32)
            for s in range(slots):
                hit = jnp.where(ids[s] == b, 1.0, hit)
            kept = jnp.concatenate([jnp.broadcast_to(hit, (BLK, LANES))] * (width // LANES), axis=1)
            new_res[b] = mine - mine.astype(jnp.bfloat16).astype(jnp.float32) * kept

    for pair in range(slots // 2):
        picked = [res[ids_ref[0, 2 * pair + h]] for h in range(2)]
        both = jnp.concatenate(picked, axis=0).astype(jnp.bfloat16)
        for r in range(replicas):
            packed[r, pair * 2 * BLK : (pair + 1) * 2 * BLK, :] = both[:, r * cols : (r + 1) * cols]

    pl.semaphore_wait(barrier, len(plane) + len(across))

    for peer in plane:
        pltpu.make_async_remote_copy(
            rows_out.at[0], rows_in.at[rep], rows_send, rows_recv, device_id=(sec, peer), device_id_type=MESH
        ).start()
    for peer in plane:
        pltpu.make_async_remote_copy(
            packed.at[peer], recv.at[rep], data_send, data_recv, device_id=(sec, peer), device_id_type=MESH
        ).start()
    recv[pl.ds(rep, 1)] = packed[pl.ds(rep, 1)]

    others = replicas - 1
    every = rows_in.at[pl.ds(0, others)]
    pltpu.make_async_copy(every, every, rows_recv).wait()
    every = recv.at[pl.ds(0, others)]
    pltpu.make_async_copy(every, every, data_recv).wait()

    row = lax.broadcasted_iota(jnp.int32, (row_count, LANES), 0)
    summed = jnp.zeros((row_count, cols), jnp.float32)
    for pair in range(replicas // 2):
        first, second = rows_in[2 * pair], rows_in[2 * pair + 1]
        lanes = lax.broadcasted_iota(jnp.int32, (1, LANES), 1)
        both = jnp.where(lanes < slots * BLK, first, second)
        hot = jnp.where(row == both, 1.0, 0.0).astype(jnp.bfloat16)
        held = recv[2 * pair : 2 * pair + 2].reshape(2 * slots * BLK, cols)
        summed = summed + jnp.dot(hot, held, preferred_element_type=jnp.float32)

    square = (summed * summed).reshape(row_count // 8, 8, cols).sum(axis=0).sum(axis=0, keepdims=True)
    sums[0] = square
    sums_a[pl.ds(rep, 1)] = square[None]
    for peer in plane:
        pltpu.make_async_remote_copy(
            sums.at[0], sums_a.at[rep], a_send, a_recv, device_id=(sec, peer), device_id_type=MESH
        ).start()
    every = sums_a.at[pl.ds(0, others)]
    pltpu.make_async_copy(every, every, a_recv).wait()
    of_plane = sums_a[...].reshape(replicas, cols).sum(axis=0, keepdims=True)
    sums[1] = of_plane
    sums_b[pl.ds(sec, 1)] = of_plane[None]
    for peer in across:
        pltpu.make_async_remote_copy(
            sums.at[1], sums_b.at[sec], b_send, b_recv, device_id=(peer, rep), device_id_type=MESH
        ).start()
    every = sums_b.at[pl.ds(0, sections - 1)]
    pltpu.make_async_copy(every, every, b_recv).wait()
    of_all = sums_b[...].reshape(sections, cols).sum(axis=0, keepdims=True).sum(axis=1, keepdims=True)
    clip_factor = scale_level / jnp.sqrt(of_all / count_total + epsilon)
    update[...] = (summed * clip_factor).astype(jnp.bfloat16)

    every = packed.at[pl.ds(0, others)]
    pltpu.make_async_copy(every, every, data_send).wait()
    every = rows_in.at[pl.ds(0, others)]
    pltpu.make_async_copy(every, every, rows_send).wait()
    every = sums_a.at[pl.ds(0, others)]
    pltpu.make_async_copy(every, every, a_send).wait()
    every = sums_b.at[pl.ds(0, sections - 1)]
    pltpu.make_async_copy(every, every, b_send).wait()


def per_device(nz, nx, sections, gradient, residual, block_ids, block_counts):
    replicas = nz * nx
    row_count, width = gradient.shape
    cols = width // replicas
    slots = block_ids.shape[1]
    count_total = sections * row_count * width
    f32, bf16, i32 = jnp.float32, jnp.bfloat16, jnp.int32
    dma = pltpu.SemaphoreType.DMA
    blocks = row_count // BLK
    shape = (blocks, BLK, width)
    new_residual, update = pl.pallas_call(
        functools.partial(kernel, nz, nx, sections, count_total),
        out_shape=(
            OUT(shape, f32),
            OUT((row_count, cols), bf16),
        ),
        in_specs=[
            pl.BlockSpec(memory_space=pl.ANY),
            pl.BlockSpec(memory_space=pl.ANY),
            pl.BlockSpec(memory_space=pltpu.SMEM),
            pl.BlockSpec(memory_space=pltpu.SMEM),
        ],
        out_specs=(
            pl.BlockSpec(memory_space=pltpu.VMEM),
            pl.BlockSpec(memory_space=pltpu.VMEM),
        ),
        scratch_shapes=[
            pltpu.VMEM(shape, bf16),
            pltpu.VMEM(shape, f32),
            pltpu.VMEM((replicas, slots * BLK, cols), bf16),
            pltpu.VMEM((1, 1, LANES), i32),
            pltpu.VMEM((replicas, slots * BLK, cols), bf16),
            pltpu.VMEM((replicas, 1, LANES), i32),
            pltpu.VMEM((2, 1, cols), f32),
            pltpu.VMEM((replicas, 1, cols), f32),
            pltpu.VMEM((sections, 1, cols), f32),
            dma((2, 4)), dma, dma, dma, dma, dma, dma, dma, dma,
        ],
        compiler_params=pltpu.CompilerParams(
            collective_id=0, has_side_effects=True
        ),
    )(gradient.reshape(shape), residual.reshape(shape), block_ids, block_counts)
    return new_residual.reshape(row_count, width), update


OUT = jax.ShapeDtypeStruct


def solution(mesh):
    sections, replicas = mesh.shape["section"], mesh.shape["replica"]
    nx = 4
    nz = replicas // nx
    both = P("section", "replica")
    return jax.shard_map(
        functools.partial(per_device, nz, nx, sections),
        mesh=mesh,
        in_specs=(both, both, both, both),
        out_specs=(both, both),
        check_vma=False,
    )
```

time: 75.6 us -> 43.3 us (0.57)
  Pallas kernels: 0 us -> 38.1 us
  blocking collectives: 27.1 us -> 0 us
  starting transfers between devices: 21.7 us -> 0 us
  waiting for transfers between devices: 7.37 us -> 0 us
  other arithmetic: 7.14 us -> 0 us
  local copies, waits for them, and re-layouts: 6.66 us -> 3.74 us
  between operations: 3.44 us -> 1.29 us
  matrix products: 1.84 us -> 0 us
    pallas_call x0 -> x1, Pallas kernels: none -> 38.1 us  [per_device(): pl.pallas_call(functools.partial(kernel, nz, nx, sections, count_total),...]
    all_to_all x2 -> x0, starting transfers between devices: 21.7 us -> none  [the longest x1 12 us: per_device(): lax.all_to_all(column_parts, REPLICA, split_axis=2, concat_axis=0, tiled=...]
    unnamed x2 -> x0, blocking collectives: 19 us -> none
    all_to_all x1 -> x0, blocking collectives: 8.12 us -> none  [sent_to_all(): return lax.all_to_all(copies, axis, split_axis=0, concat_axis=0, tiled=True)]
    all_to_all x2 -> x0, waiting for transfers between devices: 7.37 us -> none  [the longest x1 7.37 us: sent_to_all(): return lax.all_to_all(copies, axis, split_axis=0, concat_axis=0, tiled=True)]
    unnamed x16 -> x4, local copies, waits for them, and re-layouts: 1.57 us -> 3.74 us
    broadcast_in_dim x4 -> x0, local copies, waits for them, and re-layouts: 2.1 us -> none  [the longest x2 1.92 us: sent_to_all(): copies = jnp.broadcast_to(x, (lax.axis_size(axis), *x.shape))]
    reshape x1 -> x0, other arithmetic: 2.06 us -> none  [per_device(): picked = accumulated.reshape(block_total, BLK, width)[slot_ids]]
  transfers between devices with their start and end apart: 2 -> 0, of which waited for: 1 -> 0; matrix products, arithmetic and copies ran while one was open for 5% -> 0% of each run, Pallas kernels for 0% -> 0%
where the time goes in v1:
time: 43.3 us; the launch traced here: 43.2 us
  Pallas kernels  38.1 us (88%)
  local copies, waits for them, and re-layouts  3.74 us (9%)
  between operations  1.29 us (3%)
    pallas_call x1, Pallas kernels, per_device(): pl.pallas_call(functools.partial(kernel, nz, nx, sections, count_total),...  38.1 us
    unnamed x4, local copies, waits for them, and re-layouts  3.74 us

profile of v1, /device:TPU:1, one launch (start us, length us, event | category | flops | bytes accessed | tf_op | source)
XLA Modules:
  0.0 43.2 jit_solution(6673160332508494312)
XLA Ops:
  1.3 38.1 %shard_map.59 = (f32[16,8,4096]{2,1,0:T(8,128)}, bf16[128,128]{1,0:T(8,128)(2,1)}) custom-call(bf16[16,8,4096]{2,1,0:T(8,128)(2,1)} %bitcast.5, f32[16,8,4096]{2,1,0:T(8,128)} %bitcast.3, s32[1,8]{1,0:T(1,128)} %ids_ref.1, s32[1,1]{1,0:T(1,128)S(6)} %copy.8.count_ref), custom_call_target="tpu_custom_call" | custom-call | tf_op jit(solution)/shard_map/pallas_call | solution.py:162
  39.4 0.0 copy-start
  39.4 3.1 %copy.9 = f32[128,4096]{1,0:T(8,128)} copy(f32[128,4096]{1,0:T(8,128)} %bitcast.4) | data formatting | bytes 4194304
  42.6 0.0 copy-done
  42.6 0.6 %copy.10 = bf16[128,128]{1,0:T(8,128)(2,1)} copy(bf16[128,128]{1,0:T(8,128)(2,1)S(1)} %copy-done) | data formatting | bytes 65536
Async XLA Ops:
  39.4 3.1 %copy-start = (bf16[128,128]{1,0:T(8,128)(2,1)S(1)}, bf16[128,128]{1,0:T(8,128)(2,1)}, u32[]{:S(2)}) copy-start(bf16[128,128]{1,0:T(8,128)(2,1)} %get-tuple-element.9) | copy-start | bytes 98308

commit v2 on v1

v2 whole, which is shorter than its diff:
```python
import functools
import jax
import jax.numpy as jnp
from jax import lax
from jax.experimental import pallas as pl
from jax.experimental.pallas import tpu as pltpu
from jax.sharding import PartitionSpec as P

BLK = 8
LANES = 128
NX = 4
DIRECT = 4
MESH = pl.DeviceIdType.MESH

scale_level = 1.0
epsilon = 1e-06


def ring_far(d, n):
    return min(d, n - d)


def plane_order(nz, nx):
    offsets = [(dz, dx) for dz in range(nz) for dx in range(nx) if (dz, dx) != (0, 0)]
    return sorted(
        offsets, key=lambda o: (-ring_far(o[0], nz) - ring_far(o[1], nx), ring_far(o[1], nx), o)
    )


def kernel(
    nz, nx, sections, count_total,
    grad_hbm, res_hbm, ids_ref, count_ref,
    new_res, update,
    grad, res, packed, packed_ext, rows_out, recv, recv_ext, merged, recv_merged, rows_in, square_out, squares,
    load_sem, data_send, data_recv, rows_send, rows_recv, ext_send, ext_recv, merged_send, merged_recv,
    square_send, square_recv,
):
    replicas = nz * nx
    blocks, _, width = grad.shape
    row_count = blocks * BLK
    cols = width // replicas
    slots = ids_ref.shape[1]
    sec, rep = lax.axis_index("section"), lax.axis_index("replica")
    z, x = rep // nx, rep % nx
    others = replicas - 1
    f32, bf16 = jnp.float32, jnp.bfloat16

    loads = []
    chunks = 4
    step = blocks // chunks
    for c in range(chunks):
        part = pl.ds(c * step, step)
        pair = (
            pltpu.make_async_copy(grad_hbm.at[part], grad.at[part], load_sem.at[0, c]),
            pltpu.make_async_copy(res_hbm.at[part], res.at[part], load_sem.at[1, c]),
        )
        for copy in pair:
            copy.start()
        loads.append(pair)

    order = plane_order(nz, nx)
    peer_of = {(dz, dx): ((z + dz) % nz) * nx + (x + dx) % nx for dz, dx in order}
    across = [(sec + d) % sections for d in range(1, sections)]
    barrier = pltpu.get_barrier_semaphore()
    for o in order:
        pl.semaphore_signal(barrier, inc=1, device_id=(sec, peer_of[o]), device_id_type=MESH)
    for peer in across:
        pl.semaphore_signal(barrier, inc=1, device_id=(peer, rep), device_id_type=MESH)

    lane = lax.broadcasted_iota(jnp.int32, (1, LANES), 1)
    group = LANES // (DIRECT * BLK)
    slot_of = lane // BLK - (rep % group) * DIRECT
    count = jnp.full((1, LANES), count_ref[0, 0], jnp.int32)
    ids = [jnp.full((1, LANES), ids_ref[0, s], jnp.int32) for s in range(slots)]
    ids = [jnp.where(count > s, ids[s], -1) for s in range(slots)]
    direct_row = jnp.zeros((1, LANES), jnp.int32)
    ext_row = jnp.zeros((1, LANES), jnp.int32)
    for s in range(slots):
        target = jnp.where(ids[s] >= 0, ids[s] * BLK + lane % BLK + 1, 0)
        if s < DIRECT:
            direct_row = jnp.where(slot_of == s, target, direct_row)
        else:
            ext_row = jnp.where(lane // BLK == s - DIRECT, target, ext_row)
    both_rows = jnp.concatenate([direct_row, ext_row], axis=0)
    rows_out[0] = both_rows
    rows_in[pl.ds(rep, 1)] = both_rows[None]

    for c in range(chunks):
        for copy in loads[c]:
            copy.wait()
        for b in range(c * step, (c + 1) * step):
            res[b] = grad[b].astype(f32) + res[b]

    shift = nz // 2 + 1
    far_steps = 3
    for pair in range(DIRECT // 2, slots // 2):
        picked = []
        for h in range(2):
            s = 2 * pair + h
            alive = jnp.broadcast_to(jnp.where(ids[s] >= 0, 1.0, 0.0), (BLK, LANES))
            alive = jnp.concatenate([alive] * (width // LANES), axis=1)
            picked.append(jnp.where(alive > 0.5, res[ids_ref[0, s]], 0.0))
        both = jnp.concatenate(picked, axis=0).astype(bf16)
        rows = slice((pair - DIRECT // 2) * 2 * BLK, (pair - DIRECT // 2 + 1) * 2 * BLK)
        for zd in range(nz):
            place = (zd - z + shift + nz) % nz
            for xd in range(nx):
                r = zd * nx + xd
                packed_ext[xd, pl.ds(place, 1), rows, :] = both[None, :, r * cols : (r + 1) * cols]
    for pair in range(DIRECT // 2):
        both = jnp.concatenate([res[ids_ref[0, 2 * pair + h]] for h in range(2)], axis=0).astype(bf16)
        rows = slice(pair * 2 * BLK, (pair + 1) * 2 * BLK)
        for r in range(replicas):
            packed[r, rows, :] = both[:, r * cols : (r + 1) * cols]
    recv[pl.ds(rep, 1)] = packed[pl.ds(rep, 1)]
    recv_ext[pl.ds(x, 1)] = packed_ext[pl.ds(x, 1)]

    pl.semaphore_wait(barrier, len(order) + len(across))

    halves = (pl.ds(0, far_steps), pl.ds(far_steps, nz - far_steps))
    for h in range(2):
        for dx in sorted(range(1, nx), key=lambda d: -ring_far(d, nx)):
            xd = (x + dx) % nx
            pltpu.make_async_remote_copy(
                packed_ext.at[xd, halves[h]], recv_ext.at[x, halves[h]], ext_send.at[h], ext_recv.at[h],
                device_id=(sec, z * nx + xd), device_id_type=MESH,
            ).start()
    for o in order:
        pltpu.make_async_remote_copy(
            rows_out.at[0], rows_in.at[rep], rows_send, rows_recv, device_id=(sec, peer_of[o]), device_id_type=MESH
        ).start()

    def send_direct(lengths):
        for o in order:
            if ring_far(o[0], nz) in lengths:
                pltpu.make_async_remote_copy(
                    packed.at[peer_of[o]], recv.at[rep], data_send, data_recv,
                    device_id=(sec, peer_of[o]), device_id_type=MESH,
                ).start()

    def forward(h):
        places = range(far_steps) if h == 0 else range(far_steps, nz)
        every = recv_ext.at[pl.ds(0, nx - 1), halves[h]]
        pltpu.make_async_copy(every, every, ext_recv.at[h]).wait()
        total = recv_ext[0, places[0] : places[-1] + 1]
        for k in range(1, nx):
            total = total + recv_ext[k, places[0] : places[-1] + 1]
        merged[places[0] : places[-1] + 1] = total
        for place in sorted(places, key=lambda p: -ring_far((p - shift) % nz, nz)):
            dz = (place - shift) % nz
            if dz:
                pltpu.make_async_remote_copy(
                    merged.at[place], recv_merged.at[z], merged_send, merged_recv,
                    device_id=(sec, ((z + dz) % nz) * nx + x), device_id_type=MESH,
                ).start()
            else:
                recv_merged[pl.ds(z, 1)] = total[place - places[0] : place - places[0] + 1]

    send_direct((3, 4))
    forward(0)
    send_direct((2,))
    forward(1)
    send_direct((1, 0))

    for b in range(blocks):
        hit = jnp.zeros((1, LANES), f32)
        for s in range(slots):
            hit = jnp.where(ids[s] == b, 1.0, hit)
        kept = jnp.concatenate([jnp.broadcast_to(hit, (BLK, LANES))] * (width // LANES), axis=1)
        mine = res[b]
        new_res[b] = mine - mine.astype(bf16).astype(f32) * kept

    every = rows_in.at[pl.ds(0, others)]
    pltpu.make_async_copy(every, every, rows_recv).wait()
    row = lax.broadcasted_iota(jnp.int32, (row_count, LANES), 0) + 1
    ext_rows = rows_in[0][1:2]
    for r in range(1, replicas):
        ext_rows = ext_rows + rows_in[r][1:2]
    hot_ext = jnp.where(row == ext_rows, 1.0, 0.0).astype(bf16)[:, : (slots - DIRECT) * BLK]
    hots = []
    for g in range(replicas // group):
        rows = rows_in[g * group][0:1]
        for k in range(1, group):
            rows = rows + rows_in[g * group + k][0:1]
        hots.append(jnp.where(row == rows, 1.0, 0.0).astype(bf16))

    every = recv.at[pl.ds(0, others)]
    pltpu.make_async_copy(every, every, data_recv).wait()
    every = recv_merged.at[pl.ds(0, nz - 1)]
    pltpu.make_async_copy(every, every, merged_recv).wait()

    ext = recv_merged[0]
    for k in range(1, nz):
        ext = ext + recv_merged[k]
    summed = jnp.dot(hot_ext, ext, preferred_element_type=f32)
    for g, hot in enumerate(hots):
        held = recv[g * group : (g + 1) * group].reshape(LANES, cols)
        summed = summed + jnp.dot(hot, held, preferred_element_type=f32)

    square = (summed * summed).reshape(row_count // 8, 8, cols).sum(axis=0).sum(axis=0, keepdims=True)
    device = sec * replicas + rep
    square_out[0] = square
    squares[pl.ds(device, 1)] = square[None]
    for o in order:
        for d in range(sections):
            pltpu.make_async_remote_copy(
                square_out.at[0], squares.at[device], square_send, square_recv,
                device_id=((sec + d) % sections, peer_of[o]), device_id_type=MESH,
            ).start()
    for peer in across:
        pltpu.make_async_remote_copy(
            square_out.at[0], squares.at[device], square_send, square_recv,
            device_id=(peer, rep), device_id_type=MESH,
        ).start()
    every_square = squares.at[pl.ds(0, sections * replicas - 1)]
    pltpu.make_async_copy(every_square, every_square, square_recv).wait()
    of_all = squares[...].sum(axis=0).sum(axis=1, keepdims=True)
    clip_factor = scale_level / jnp.sqrt(of_all / count_total + epsilon)
    update[...] = (summed * clip_factor).astype(bf16)

    every = packed.at[pl.ds(0, others)]
    pltpu.make_async_copy(every, every, data_send).wait()
    every = rows_in.at[pl.ds(0, others)]
    pltpu.make_async_copy(every, every, rows_send).wait()
    for h in range(2):
        every = recv_ext.at[pl.ds(0, nx - 1), halves[h]]
        pltpu.make_async_copy(every, every, ext_send.at[h]).wait()
    every = recv_merged.at[pl.ds(0, nz - 1)]
    pltpu.make_async_copy(every, every, merged_send).wait()
    pltpu.make_async_copy(every_square, every_square, square_send).wait()


def per_device(nz, nx, sections, gradient, residual, block_ids, block_counts):
    replicas = nz * nx
    row_count, width = gradient.shape
    cols = width // replicas
    slots = block_ids.shape[1]
    count_total = sections * row_count * width
    f32, bf16, i32 = jnp.float32, jnp.bfloat16, jnp.int32
    dma = pltpu.SemaphoreType.DMA
    blocks = row_count // BLK
    shape = (blocks, BLK, width)
    direct_rows, ext_rows = DIRECT * BLK, (slots - DIRECT) * BLK
    new_residual, update = pl.pallas_call(
        functools.partial(kernel, nz, nx, sections, count_total),
        out_shape=(pltpu.VMEM(shape, f32), pltpu.VMEM((row_count, cols), bf16)),
        in_specs=[
            pl.BlockSpec(memory_space=pl.ANY),
            pl.BlockSpec(memory_space=pl.ANY),
            pl.BlockSpec(memory_space=pltpu.SMEM),
            pl.BlockSpec(memory_space=pltpu.SMEM),
        ],
        out_specs=(
            pl.BlockSpec(memory_space=pltpu.VMEM),
            pl.BlockSpec(memory_space=pltpu.VMEM),
        ),
        scratch_shapes=[
            pltpu.VMEM(shape, bf16),
            pltpu.VMEM(shape, f32),
            pltpu.VMEM((replicas, direct_rows, cols), bf16),
            pltpu.VMEM((nx, nz, ext_rows, cols), bf16),
            pltpu.VMEM((1, 2, LANES), i32),
            pltpu.VMEM((replicas, direct_rows, cols), bf16),
            pltpu.VMEM((nx, nz, ext_rows, cols), bf16),
            pltpu.VMEM((nz, ext_rows, cols), bf16),
            pltpu.VMEM((nz, ext_rows, cols), bf16),
            pltpu.VMEM((replicas, 2, LANES), i32),
            pltpu.VMEM((1, 1, cols), f32),
            pltpu.VMEM((sections * replicas, 1, cols), f32),
            dma((2, 4)), dma, dma, dma, dma, dma((2,)), dma((2,)), dma, dma, dma, dma,
        ],
        compiler_params=pltpu.CompilerParams(collective_id=0, has_side_effects=True),
    )(gradient.reshape(shape), residual.reshape(shape), block_ids, block_counts)
    return new_residual.reshape(row_count, width), update


def solution(mesh):
    sections, replicas = mesh.shape["section"], mesh.shape["replica"]
    both = P("section", "replica")
    return jax.shard_map(
        functools.partial(per_device, replicas // NX, NX, sections),
        mesh=mesh,
        in_specs=(both, both, both, both),
        out_specs=(both, both),
        check_vma=False,
    )
```

time: 43.3 us -> 35 us (0.81)
  Pallas kernels: 38.1 us -> 31.7 us
  local copies, waits for them, and re-layouts: 3.74 us -> 1.94 us
    pallas_call x1, Pallas kernels: 38.1 us -> 31.7 us  [per_device(): pl.pallas_call(functools.partial(kernel, nz, nx, sections, count_total),...]
    unnamed x4 -> x2, local copies, waits for them, and re-layouts: 3.74 us -> 1.94 us
where the time goes in v2:
time: 35 us; the launch traced here: 34.9 us
  Pallas kernels  31.7 us (91%)
  local copies, waits for them, and re-layouts  1.94 us (6%)
  between operations  1.29 us (4%)
    pallas_call x1, Pallas kernels, per_device(): pl.pallas_call(functools.partial(kernel, nz, nx, sections, count_total),...  31.7 us
    unnamed x2, local copies, waits for them, and re-layouts  1.94 us

profile of v2, /device:TPU:1, one launch (start us, length us, event | category | flops | bytes accessed | tf_op | source)
XLA Modules:
  0.0 34.9 jit_solution(8191509044710064645)
XLA Ops:
  1.3 31.7 %shard_map.59 = (f32[16,8,4096]{2,1,0:T(8,128)S(1)}, bf16[128,128]{1,0:T(8,128)(2,1)S(1)}) custom-call(bf16[16,8,4096]{2,1,0:T(8,128)(2,1)} %bitcast.5, f32[16,8,4096]{2,1,0:T(8,128)} %bitcast.4, s32[1,8]{1,0:T(1,128)} %ids_ref.1, s32[1,1]{1,0:T(1,128)S(6)} %copy.10.count_ref), custom_call_target="tpu_custom_call" | custom-call | tf_op jit(solution)/shard_map/pallas_call | solution.py:244
  32.9 1.3 %copy.8 = f32[128,4096]{1,0:T(8,128)} copy(f32[128,4096]{1,0:T(8,128)S(1)} %bitcast.3) | data formatting | bytes 4194304
  34.3 0.6 %copy.9 = bf16[128,128]{1,0:T(8,128)(2,1)} copy(bf16[128,128]{1,0:T(8,128)(2,1)S(1)} %get-tuple-element.7) | data formatting | bytes 65536

commit v3 on v2

--- a/solution.py
+++ b/solution.py
@@ -28,10 +28,10 @@
 
 
 def kernel(
-    nz, nx, sections, count_total,
+    nz, nx, sections,
     grad_hbm, res_hbm, ids_ref, count_ref,
-    new_res, update,
-    grad, res, packed, packed_ext, rows_out, recv, recv_ext, merged, recv_merged, rows_in, square_out, squares,
+    new_res, summed_out, squares,
+    grad, res, packed, packed_ext, rows_out, recv, recv_ext, merged, recv_merged, rows_in, square_out,
     load_sem, data_send, data_recv, rows_send, rows_recv, ext_send, ext_recv, merged_send, merged_recv,
     square_send, square_recv,
 ):
@@ -73,17 +73,16 @@
     count = jnp.full((1, LANES), count_ref[0, 0], jnp.int32)
     ids = [jnp.full((1, LANES), ids_ref[0, s], jnp.int32) for s in range(slots)]
     ids = [jnp.where(count > s, ids[s], -1) for s in range(slots)]
-    direct_row = jnp.zeros((1, LANES), jnp.int32)
-    ext_row = jnp.zeros((1, LANES), jnp.int32)
+    base = 2 * row_count
+    both_rows = jnp.zeros((1, LANES), jnp.int32)
     for s in range(slots):
         target = jnp.where(ids[s] >= 0, ids[s] * BLK + lane % BLK + 1, 0)
         if s < DIRECT:
-            direct_row = jnp.where(slot_of == s, target, direct_row)
+            both_rows = both_rows + jnp.where(slot_of == s, target, 0)
         else:
-            ext_row = jnp.where(lane // BLK == s - DIRECT, target, ext_row)
-    both_rows = jnp.concatenate([direct_row, ext_row], axis=0)
-    rows_out[0] = both_rows
-    rows_in[pl.ds(rep, 1)] = both_rows[None]
+            both_rows = both_rows + jnp.where(slot_of == s - DIRECT, target * base, 0)
+    rows_out[...] = both_rows
+    rows_in[pl.ds(rep, 1)] = both_rows
 
     for c in range(chunks):
         for copy in loads[c]:
@@ -127,7 +126,7 @@
             ).start()
     for o in order:
         pltpu.make_async_remote_copy(
-            rows_out.at[0], rows_in.at[rep], rows_send, rows_recv, device_id=(sec, peer_of[o]), device_id_type=MESH
+            rows_out, rows_in.at[pl.ds(rep, 1)], rows_send, rows_recv, device_id=(sec, peer_of[o]), device_id_type=MESH
         ).start()
 
     def send_direct(lengths):
@@ -173,16 +172,11 @@
     every = rows_in.at[pl.ds(0, others)]
     pltpu.make_async_copy(every, every, rows_recv).wait()
     row = lax.broadcasted_iota(jnp.int32, (row_count, LANES), 0) + 1
-    ext_rows = rows_in[0][1:2]
-    for r in range(1, replicas):
-        ext_rows = ext_rows + rows_in[r][1:2]
-    hot_ext = jnp.where(row == ext_rows, 1.0, 0.0).astype(bf16)[:, : (slots - DIRECT) * BLK]
-    hots = []
-    for g in range(replicas // group):
-        rows = rows_in[g * group][0:1]
-        for k in range(1, group):
-            rows = rows + rows_in[g * group + k][0:1]
-        hots.append(jnp.where(row == rows, 1.0, 0.0).astype(bf16))
+    lists = rows_in[...]
+    ext_rows = (lists // base).sum(axis=0, keepdims=True)
+    direct_rows = (lists % base).reshape(replicas // group, group, LANES).sum(axis=1)
+    hot_ext = jnp.where(row == ext_rows, 1.0, 0.0).astype(bf16)
+    hots = [jnp.where(row == direct_rows[g : g + 1], 1.0, 0.0).astype(bf16) for g in range(replicas // group)]
 
     every = recv.at[pl.ds(0, others)]
     pltpu.make_async_copy(every, every, data_recv).wait()
@@ -192,32 +186,28 @@
     ext = recv_merged[0]
     for k in range(1, nz):
         ext = ext + recv_merged[k]
-    summed = jnp.dot(hot_ext, ext, preferred_element_type=f32)
+    summed = jnp.dot(hot_ext, jnp.concatenate([ext] * group, axis=0), preferred_element_type=f32)
     for g, hot in enumerate(hots):
         held = recv[g * group : (g + 1) * group].reshape(LANES, cols)
         summed = summed + jnp.dot(hot, held, preferred_element_type=f32)
 
-    square = (summed * summed).reshape(row_count // 8, 8, cols).sum(axis=0).sum(axis=0, keepdims=True)
+    summed_out[...] = summed
     device = sec * replicas + rep
-    square_out[0] = square
-    squares[pl.ds(device, 1)] = square[None]
+    square_out[...] = (summed * summed).reshape(row_count // 8, 8, cols).sum(axis=0).sum(axis=0, keepdims=True)
+    squares[pl.ds(device, 1)] = square_out[...]
     for o in order:
         for d in range(sections):
             pltpu.make_async_remote_copy(
-                square_out.at[0], squares.at[device], square_send, square_recv,
+                square_out, squares.at[pl.ds(device, 1)], square_send, square_recv,
                 device_id=((sec + d) % sections, peer_of[o]), device_id_type=MESH,
             ).start()
     for peer in across:
         pltpu.make_async_remote_copy(
-            square_out.at[0], squares.at[device], square_send, square_recv,
+            square_out, squares.at[pl.ds(device, 1)], square_send, square_recv,
             device_id=(peer, rep), device_id_type=MESH,
         ).start()
     every_square = squares.at[pl.ds(0, sections * replicas - 1)]
     pltpu.make_async_copy(every_square, every_square, square_recv).wait()
-    of_all = squares[...].sum(axis=0).sum(axis=1, keepdims=True)
-    clip_factor = scale_level / jnp.sqrt(of_all / count_total + epsilon)
-    update[...] = (summed * clip_factor).astype(bf16)
-
     every = packed.at[pl.ds(0, others)]
     pltpu.make_async_copy(every, every, data_send).wait()
     every = rows_in.at[pl.ds(0, others)]
@@ -228,6 +218,24 @@
     every = recv_merged.at[pl.ds(0, nz - 1)]
     pltpu.make_async_copy(every, every, merged_send).wait()
     pltpu.make_async_copy(every_square, every_square, square_send).wait()
+
+
+def finish(count_total, new_res, summed, squares, new_res_hbm, update_hbm, update, res_sem, update_sem):
+    step = new_res.shape[0] // 4
+    copies = [
+        pltpu.make_async_copy(new_res.at[pl.ds(c * step, step)], new_res_hbm.at[pl.ds(c * step, step)], res_sem.at[c])
+        for c in range(4)
+    ]
+    for copy in copies:
+        copy.start()
+    every = squares[...]
+    norm_total = every.sum(axis=0, keepdims=True).sum(axis=1, keepdims=True)
+    clip_factor = scale_level / jnp.sqrt(norm_total / count_total + epsilon)
+    update[...] = (summed[...] * clip_factor).astype(jnp.bfloat16)
+    copies.append(pltpu.make_async_copy(update, update_hbm, update_sem))
+    copies[-1].start()
+    for copy in copies:
+        copy.wait()
 
 
 def per_device(nz, nx, sections, gradient, residual, block_ids, block_counts):
@@ -241,36 +249,43 @@
     blocks = row_count // BLK
     shape = (blocks, BLK, width)
     direct_rows, ext_rows = DIRECT * BLK, (slots - DIRECT) * BLK
-    new_residual, update = pl.pallas_call(
-        functools.partial(kernel, nz, nx, sections, count_total),
-        out_shape=(pltpu.VMEM(shape, f32), pltpu.VMEM((row_count, cols), bf16)),
+    new_residual, summed, squares = pl.pallas_call(
+        functools.partial(kernel, nz, nx, sections),
+        out_shape=(
+            pltpu.VMEM(shape, f32), pltpu.VMEM((row_count, cols), f32), pltpu.VMEM((sections * replicas, cols), f32)
+        ),
         in_specs=[
             pl.BlockSpec(memory_space=pl.ANY),
             pl.BlockSpec(memory_space=pl.ANY),
             pl.BlockSpec(memory_space=pltpu.SMEM),
             pl.BlockSpec(memory_space=pltpu.SMEM),
         ],
-        out_specs=(
-            pl.BlockSpec(memory_space=pltpu.VMEM),
-            pl.BlockSpec(memory_space=pltpu.VMEM),
-        ),
+        out_specs=(pl.BlockSpec(memory_space=pltpu.VMEM),) * 3,
         scratch_shapes=[
             pltpu.VMEM(shape, bf16),
             pltpu.VMEM(shape, f32),
             pltpu.VMEM((replicas, direct_rows, cols), bf16),
             pltpu.VMEM((nx, nz, ext_rows, cols), bf16),
-            pltpu.VMEM((1, 2, LANES), i32),
+            pltpu.VMEM((1, LANES), i32),
             pltpu.VMEM((replicas, direct_rows, cols), bf16),
             pltpu.VMEM((nx, nz, ext_rows, cols), bf16),
             pltpu.VMEM((nz, ext_rows, cols), bf16),
             pltpu.VMEM((nz, ext_rows, cols), bf16),
-            pltpu.VMEM((replicas, 2, LANES), i32),
-            pltpu.VMEM((1, 1, cols), f32),
-            pltpu.VMEM((sections * replicas, 1, cols), f32),
+            pltpu.VMEM((replicas, LANES), i32),
+            pltpu.VMEM((1, cols), f32),
             dma((2, 4)), dma, dma, dma, dma, dma((2,)), dma((2,)), dma, dma, dma, dma,
         ],
         compiler_params=pltpu.CompilerParams(collective_id=0, has_side_effects=True),
     )(gradient.reshape(shape), residual.reshape(shape), block_ids, block_counts)
+    any_space = pl.BlockSpec(memory_space=pltpu.HBM)
+    in_vmem = pl.BlockSpec(memory_space=pltpu.VMEM)
+    new_residual, update = pl.pallas_call(
+        functools.partial(finish, count_total),
+        out_shape=(pltpu.HBM(shape, f32), pltpu.HBM((row_count, cols), bf16)),
+        in_specs=[in_vmem] * 3,
+        out_specs=(any_space, any_space),
+        scratch_shapes=[pltpu.VMEM((row_count, cols), bf16), dma((4,)), dma],
+    )(*(pltpu.with_memory_space_constraint(v, pltpu.VMEM) for v in (new_residual, summed, squares)))
     return new_residual.reshape(row_count, width), update
 
 

time: 35 us -> 33.9 us (0.969)
  local copies, waits for them, and re-layouts: 1.94 us -> 0 us
  Pallas kernels: 31.7 us -> 32.5 us
    unnamed x2 -> x0, local copies, waits for them, and re-layouts: 1.94 us -> none
    pallas_call x1 -> x2, Pallas kernels: 31.7 us -> 32.5 us  [the longest x1 31.2 us: per_device(): pl.pallas_call(functools.partial(kernel, nz, nx, sections), out_shape=(pl...]
where the time goes in v3:
time: 33.9 us; the launch traced here: 33.8 us
  Pallas kernels  32.5 us (96%)
  between operations  1.28 us (4%)
    pallas_call x1, Pallas kernels, per_device(): pl.pallas_call(functools.partial(kernel, nz, nx, sections), out_shape=(pl...  31.2 us
    pallas_call x1, Pallas kernels, per_device(): pl.pallas_call(functools.partial(finish, count_total), out_shape=(pltpu.H...  1.36 us

profile of v3, /device:TPU:1, one launch (start us, length us, event | category | flops | bytes accessed | tf_op | source)
XLA Modules:
  0.0 33.8 jit_solution(12020919112896465593)
XLA Ops:
  1.3 31.2 %shard_map.59 = (f32[16,8,4096]{2,1,0:T(8,128)S(1)}, f32[128,128]{1,0:T(8,128)S(1)}, f32[256,128]{1,0:T(8,128)S(1)}) custom-call(bf16[16,8,4096]{2,1,0:T(8,128)(2,1)} %bitcast.4, f32[16,8,4096]{2,1,0:T(8,128)} %bitcast.3, s32[1,8]{1,0:T(1,128)} %ids_ref.1, s32[1,1]{1,0:T(1,128)S(6)} %copy.6.count_ref), custom_call_target="tpu_custom_call" | custom-call | tf_op jit(solution)/shard_map/pallas_call | solution.py:252
  32.5 1.4 %shard_map.60 = (f32[16,8,4096]{2,1,0:T(8,128)}, bf16[128,128]{1,0:T(8,128)(2,1)}) custom-call(f32[16,8,4096]{2,1,0:T(8,128)S(1)} %get-tuple-element.7.new_res, f32[128,128]{1,0:T(8,128)S(1)} %get-tuple-element.8.summed, f32[256,128]{1,0:T(8,128)S(1)} %get-tuple-element.9.squares), custom_call_target="tpu_custom_call" | custom-call | tf_op jit(solution)/shard_map/pallas_call | solution.py:282

commit v4 on v3

--- a/solution.py
+++ b/solution.py
@@ -29,10 +29,10 @@
 
 def kernel(
     nz, nx, sections,
-    grad_hbm, res_hbm, ids_ref, count_ref,
+    grad_hbm, res_hbm, ids_hbm, count_in,
     new_res, summed_out, squares,
-    grad, res, packed, packed_ext, rows_out, recv, recv_ext, merged, recv_merged, rows_in, square_out,
-    load_sem, data_send, data_recv, rows_send, rows_recv, ext_send, ext_recv, merged_send, merged_recv,
+    grad, res, packed, packed_ext, rows_out, recv, recv_ext, merged, recv_merged, rows_in, square_out, ids_ref,
+    list_sem, load_sem, data_send, data_recv, rows_send, rows_recv, ext_send, ext_recv, merged_send, merged_recv,
     square_send, square_recv,
 ):
     replicas = nz * nx
@@ -45,6 +45,8 @@
     others = replicas - 1
     f32, bf16 = jnp.float32, jnp.bfloat16
 
+    ids_copy = pltpu.make_async_copy(ids_hbm, ids_ref, list_sem)
+    ids_copy.start()
     loads = []
     chunks = 4
     step = blocks // chunks
@@ -67,10 +69,11 @@
     for peer in across:
         pl.semaphore_signal(barrier, inc=1, device_id=(peer, rep), device_id_type=MESH)
 
+    ids_copy.wait()
     lane = lax.broadcasted_iota(jnp.int32, (1, LANES), 1)
     group = LANES // (DIRECT * BLK)
     slot_of = lane // BLK - (rep % group) * DIRECT
-    count = jnp.full((1, LANES), count_ref[0, 0], jnp.int32)
+    count = jnp.broadcast_to(count_in[...], (1, LANES))
     ids = [jnp.full((1, LANES), ids_ref[0, s], jnp.int32) for s in range(slots)]
     ids = [jnp.where(count > s, ids[s], -1) for s in range(slots)]
     base = 2 * row_count
@@ -129,13 +132,28 @@
             rows_out, rows_in.at[pl.ds(rep, 1)], rows_send, rows_recv, device_id=(sec, peer_of[o]), device_id_type=MESH
         ).start()
 
-    def send_direct(lengths):
-        for o in order:
-            if ring_far(o[0], nz) in lengths:
-                pltpu.make_async_remote_copy(
-                    packed.at[peer_of[o]], recv.at[rep], data_send, data_recv,
-                    device_id=(sec, peer_of[o]), device_id_type=MESH,
-                ).start()
+    def send_to(zt, dx):
+        to = zt * nx + (x + dx) % nx
+        pltpu.make_async_remote_copy(
+            packed.at[to], recv.at[rep], data_send, data_recv, device_id=(sec, to), device_id_type=MESH
+        ).start()
+
+    half = nz // 2
+    mine_half, other_half = (z // half) * half, (1 - z // half) * half
+    cross = [other_half + (z + k) % half for k in (2, 1, 3, 0)]
+    inner = [mine_half + (z + k) % half for k in (2, 1, 3)]
+
+    def send_cross():
+        for dx in (2, 1, 3, 0):
+            for zt in cross:
+                send_to(zt, dx)
+
+    def send_inner():
+        for dx in (2, 1, 3, 0):
+            for zt in inner:
+                send_to(zt, dx)
+        for dx in (2, 1, 3):
+            send_to(z, dx)
 
     def forward(h):
         places = range(far_steps) if h == 0 else range(far_steps, nz)
@@ -155,11 +173,10 @@
             else:
                 recv_merged[pl.ds(z, 1)] = total[place - places[0] : place - places[0] + 1]
 
-    send_direct((3, 4))
+    send_cross()
     forward(0)
-    send_direct((2,))
+    send_inner()
     forward(1)
-    send_direct((1, 0))
 
     for b in range(blocks):
         hit = jnp.zeros((1, LANES), f32)
@@ -195,17 +212,22 @@
     device = sec * replicas + rep
     square_out[...] = (summed * summed).reshape(row_count // 8, 8, cols).sum(axis=0).sum(axis=0, keepdims=True)
     squares[pl.ds(device, 1)] = square_out[...]
-    for o in order:
-        for d in range(sections):
-            pltpu.make_async_remote_copy(
-                square_out, squares.at[pl.ds(device, 1)], square_send, square_recv,
-                device_id=((sec + d) % sections, peer_of[o]), device_id_type=MESH,
-            ).start()
-    for peer in across:
+    def send_square(s_to, r_to):
         pltpu.make_async_remote_copy(
             square_out, squares.at[pl.ds(device, 1)], square_send, square_recv,
-            device_id=(peer, rep), device_id_type=MESH,
+            device_id=(s_to, r_to), device_id_type=MESH,
         ).start()
+    spread = sorted(
+        [(d, dx) for d in range(sections) for dx in range(nx)],
+        key=lambda o: (-ring_far(o[0] // 2, sections // 2) - ring_far(o[1], nx), o),
+    )
+    for zt in (0, 1, 2, 3, 7, 6, 5, 4):
+        for d, dx in spread:
+            go = functools.partial(send_square, (sec + d) % sections, zt * nx + (x + dx) % nx)
+            if (d, dx) == (0, 0):
+                pl.when(z != zt)(go)
+            else:
+                go()
     every_square = squares.at[pl.ds(0, sections * replicas - 1)]
     pltpu.make_async_copy(every_square, every_square, square_recv).wait()
     every = packed.at[pl.ds(0, others)]
@@ -220,22 +242,75 @@
     pltpu.make_async_copy(every_square, every_square, square_send).wait()
 
 
-def finish(count_total, new_res, summed, squares, new_res_hbm, update_hbm, update, res_sem, update_sem):
+def released_first(nx):
+    sec, rep = lax.axis_index("section"), lax.axis_index("replica")
+    y, z, x = sec // 2, rep // nx, rep % nx
+    return y + z + jnp.minimum(x, 1) <= 1
+
+
+def ahead(nx, grad_hbm, res_hbm, ids_hbm, count_ref, new_res_hbm, grad, res, ids_ref, list_sem, load_sem, store_sem):
+    @pl.when(released_first(nx))
+    def _():
+        blocks, _, width = grad.shape
+        step = blocks // 4
+        parts = [pl.ds(c * step, step) for c in range(4)]
+        loads = [
+            (
+                pltpu.make_async_copy(grad_hbm.at[p], grad.at[p], load_sem.at[0, c]),
+                pltpu.make_async_copy(res_hbm.at[p], res.at[p], load_sem.at[1, c]),
+            )
+            for c, p in enumerate(parts)
+        ]
+        stores = [pltpu.make_async_copy(res.at[p], new_res_hbm.at[p], store_sem.at[c]) for c, p in enumerate(parts)]
+        for pair in loads:
+            for copy in pair:
+                copy.start()
+        ids_copy = pltpu.make_async_copy(ids_hbm, ids_ref, list_sem)
+        ids_copy.start()
+        ids_copy.wait()
+        count = jnp.full((1, LANES), count_ref[0, 0], jnp.int32)
+        ids = [jnp.full((1, LANES), ids_ref[0, s], jnp.int32) for s in range(ids_ref.shape[1])]
+        for c in range(4):
+            for copy in loads[c]:
+                copy.wait()
+            for b in range(c * step, (c + 1) * step):
+                hit = jnp.zeros((1, LANES), jnp.float32)
+                for s, one in enumerate(ids):
+                    hit = jnp.where((one == b) & (count > s), 1.0, hit)
+                kept = jnp.concatenate([jnp.broadcast_to(hit, (BLK, LANES))] * (width // LANES), axis=1)
+                mine = grad[b].astype(jnp.float32) + res[b]
+                res[b] = mine - mine.astype(jnp.bfloat16).astype(jnp.float32) * kept
+            stores[c].start()
+        for copy in stores:
+            copy.wait()
+
+
+def finish(count_total, nx, new_res, summed, squares, _, new_res_hbm, update_hbm, update, res_sem, update_sem):
     step = new_res.shape[0] // 4
     copies = [
         pltpu.make_async_copy(new_res.at[pl.ds(c * step, step)], new_res_hbm.at[pl.ds(c * step, step)], res_sem.at[c])
         for c in range(4)
     ]
-    for copy in copies:
-        copy.start()
+    late = jnp.logical_not(released_first(nx))
+
+    @pl.when(late)
+    def _():
+        for copy in copies:
+            copy.start()
+
     every = squares[...]
     norm_total = every.sum(axis=0, keepdims=True).sum(axis=1, keepdims=True)
     clip_factor = scale_level / jnp.sqrt(norm_total / count_total + epsilon)
     update[...] = (summed[...] * clip_factor).astype(jnp.bfloat16)
-    copies.append(pltpu.make_async_copy(update, update_hbm, update_sem))
-    copies[-1].start()
-    for copy in copies:
-        copy.wait()
+    last = pltpu.make_async_copy(update, update_hbm, update_sem)
+    last.start()
+
+    @pl.when(late)
+    def _():
+        for copy in copies:
+            copy.wait()
+
+    last.wait()
 
 
 def per_device(nz, nx, sections, gradient, residual, block_ids, block_counts):
@@ -249,17 +324,23 @@
     blocks = row_count // BLK
     shape = (blocks, BLK, width)
     direct_rows, ext_rows = DIRECT * BLK, (slots - DIRECT) * BLK
+    gradient, residual = gradient.reshape(shape), residual.reshape(shape)
+    in_hbm = pl.BlockSpec(memory_space=pltpu.HBM)
+    in_vmem = pl.BlockSpec(memory_space=pltpu.VMEM)
+    in_smem = pl.BlockSpec(memory_space=pltpu.SMEM)
+    early_residual = pl.pallas_call(
+        functools.partial(ahead, nx),
+        out_shape=pltpu.HBM(shape, f32),
+        in_specs=[in_hbm, in_hbm, in_hbm, in_smem],
+        out_specs=in_hbm,
+        scratch_shapes=[pltpu.VMEM(shape, bf16), pltpu.VMEM(shape, f32), pltpu.SMEM((1, slots), i32), dma, dma((2, 4)), dma((4,))],
+    )(gradient, residual, block_ids, block_counts)
     new_residual, summed, squares = pl.pallas_call(
         functools.partial(kernel, nz, nx, sections),
         out_shape=(
             pltpu.VMEM(shape, f32), pltpu.VMEM((row_count, cols), f32), pltpu.VMEM((sections * replicas, cols), f32)
         ),
-        in_specs=[
-            pl.BlockSpec(memory_space=pl.ANY),
-            pl.BlockSpec(memory_space=pl.ANY),
-            pl.BlockSpec(memory_space=pltpu.SMEM),
-            pl.BlockSpec(memory_space=pltpu.SMEM),
-        ],
+        in_specs=[pl.BlockSpec(memory_space=pltpu.HBM)] * 3 + [pl.BlockSpec(memory_space=pltpu.VMEM)],
         out_specs=(pl.BlockSpec(memory_space=pltpu.VMEM),) * 3,
         scratch_shapes=[
             pltpu.VMEM(shape, bf16),
@@ -273,19 +354,20 @@
             pltpu.VMEM((nz, ext_rows, cols), bf16),
             pltpu.VMEM((replicas, LANES), i32),
             pltpu.VMEM((1, cols), f32),
-            dma((2, 4)), dma, dma, dma, dma, dma((2,)), dma((2,)), dma, dma, dma, dma,
+            pltpu.SMEM((1, slots), i32),
+            dma, dma((2, 4)), dma, dma, dma, dma, dma((2,)), dma((2,)), dma, dma, dma, dma,
         ],
         compiler_params=pltpu.CompilerParams(collective_id=0, has_side_effects=True),
-    )(gradient.reshape(shape), residual.reshape(shape), block_ids, block_counts)
-    any_space = pl.BlockSpec(memory_space=pltpu.HBM)
-    in_vmem = pl.BlockSpec(memory_space=pltpu.VMEM)
+    )(gradient, residual, block_ids, block_counts)
+    parts = (pltpu.with_memory_space_constraint(v, pltpu.VMEM) for v in (new_residual, summed, squares))
     new_residual, update = pl.pallas_call(
-        functools.partial(finish, count_total),
+        functools.partial(finish, count_total, nx),
         out_shape=(pltpu.HBM(shape, f32), pltpu.HBM((row_count, cols), bf16)),
-        in_specs=[in_vmem] * 3,
-        out_specs=(any_space, any_space),
+        in_specs=[in_vmem] * 3 + [in_hbm],
+        out_specs=(in_hbm, in_hbm),
         scratch_shapes=[pltpu.VMEM((row_count, cols), bf16), dma((4,)), dma],
-    )(*(pltpu.with_memory_space_constraint(v, pltpu.VMEM) for v in (new_residual, summed, squares)))
+        input_output_aliases={3: 0},
+    )(*parts, early_residual)
     return new_residual.reshape(row_count, width), update
 
 

time: 33.9 us -> 32 us (0.944)
  Pallas kernels: 32.5 us -> 30.6 us
    pallas_call x1, Pallas kernels: 31.2 us -> 27 us  [per_device(): pl.pallas_call(functools.partial(kernel, nz, nx, sections), out_shape=(pl...]
    pallas_call x1 -> x2, Pallas kernels: 1.36 us -> 3.68 us  [the longest x1 2.88 us: per_device(): pl.pallas_call(functools.partial(ahead, nx), out_shape=pltpu.HBM(shape, f...]
where the time goes in v4:
time: 32 us; the launch traced here: 31.9 us
  Pallas kernels  30.6 us (96%)
  between operations  1.29 us (4%)
    pallas_call x1, Pallas kernels, per_device(): pl.pallas_call(functools.partial(kernel, nz, nx, sections), out_shape=(pl...  27 us
    pallas_call x1, Pallas kernels, per_device(): pl.pallas_call(functools.partial(ahead, nx), out_shape=pltpu.HBM(shape, f...  2.88 us
    pallas_call x1, Pallas kernels, per_device(): pl.pallas_call(functools.partial(finish, count_total, nx), out_shape=(plt...  0.8 us

profile of v4, /device:TPU:1, one launch (start us, length us, event | category | flops | bytes accessed | tf_op | source)
XLA Modules:
  0.0 31.9 jit_solution(12541954656532544985)
XLA Ops:
  1.3 2.9 %shard_map.60._ = f32[16,8,4096]{2,1,0:T(8,128)} custom-call(bf16[16,8,4096]{2,1,0:T(8,128)(2,1)} %bitcast.6, f32[16,8,4096]{2,1,0:T(8,128)} %bitcast.3, s32[1,8]{1,0:T(1,128)} %ids_hbm.3, s32[1,1]{1,0:T(1,128)S(6)} %copy.8.count_in.count_ref), custom_call_target="tpu_custom_call" | custom-call | tf_op jit(solution)/shard_map/pallas_call | solution.py:331
  4.2 27.0 %shard_map.59 = (f32[16,8,4096]{2,1,0:T(8,128)S(1)}, f32[128,128]{1,0:T(8,128)S(1)}, f32[256,128]{1,0:T(8,128)S(1)}) custom-call(bf16[16,8,4096]{2,1,0:T(8,128)(2,1)} %bitcast.7, f32[16,8,4096]{2,1,0:T(8,128)} %bitcast.4, s32[1,8]{1,0:T(1,128)} %ids_hbm.3, s32[1,1]{1,0:T(1,128)S(6)} %copy.8.count_in.count_ref), custom_call_target="tpu_custom_call" | custom-call | tf_op jit(solution)/shard_map/pallas_call | solution.py:338
  31.1 0.8 %shard_map.61 = (f32[16,8,4096]{2,1,0:T(8,128)}, bf16[128,128]{1,0:T(8,128)(2,1)}) custom-call(f32[16,8,4096]{2,1,0:T(8,128)S(1)} %get-tuple-element.7.new_res, f32[128,128]{1,0:T(8,128)S(1)} %get-tuple-element.8.summed, f32[256,128]{1,0:T(8,128)S(1)} %get-tuple-element.9.squares, f32[16,8,4096]{2,1,0:T(8,128)} %shard_map.60._), custom_call_target="tpu_custom_call", output_to_operand_aliasing={{0}: (3, {})} | custom-call | tf_op jit(solution)/shard_map/pallas_call | solution.py:363

commit v5 on v4

--- a/solution.py
+++ b/solution.py
@@ -20,19 +20,12 @@
     return min(d, n - d)
 
 
-def plane_order(nz, nx):
-    offsets = [(dz, dx) for dz in range(nz) for dx in range(nx) if (dz, dx) != (0, 0)]
-    return sorted(
-        offsets, key=lambda o: (-ring_far(o[0], nz) - ring_far(o[1], nx), ring_far(o[1], nx), o)
-    )
-
-
 def kernel(
     nz, nx, sections,
     grad_hbm, res_hbm, ids_hbm, count_in,
     new_res, summed_out, squares,
-    grad, res, packed, packed_ext, rows_out, recv, recv_ext, merged, recv_merged, rows_in, square_out, ids_ref,
-    list_sem, load_sem, data_send, data_recv, rows_send, rows_recv, ext_send, ext_recv, merged_send, merged_recv,
+    grad, res, packed, packed_ext, rows_out, recv, recv_ext, merged, recv_merged, rows_x, rows_in, square_out, ids_ref,
+    column_in, list_sem, load_sem, data_send, data_recv, rows_x_send, rows_x_recv, rows_send, rows_recv, ext_send, ext_recv, merged_send, merged_recv,
     square_send, square_recv,
 ):
     replicas = nz * nx
@@ -44,6 +37,15 @@
     z, x = rep // nx, rep % nx
     others = replicas - 1
     f32, bf16 = jnp.float32, jnp.bfloat16
+
+    column = [((z + d) % nz) * nx + x for d in sorted(range(1, nz), key=lambda d: -ring_far(d, nz))]
+    line = {dx: z * nx + (x + dx) % nx for dx in (2, 1, 3)}
+    across = [(sec + d) % sections for d in range(1, sections)]
+    barrier = pltpu.get_barrier_semaphore()
+    for peer in column + list(line.values()):
+        pl.semaphore_signal(barrier, inc=1, device_id=(sec, peer), device_id_type=MESH)
+    for peer in across:
+        pl.semaphore_signal(barrier, inc=1, device_id=(peer, rep), device_id_type=MESH)
 
     ids_copy = pltpu.make_async_copy(ids_hbm, ids_ref, list_sem)
     ids_copy.start()
@@ -59,15 +61,6 @@
         for copy in pair:
             copy.start()
         loads.append(pair)
-
-    order = plane_order(nz, nx)
-    peer_of = {(dz, dx): ((z + dz) % nz) * nx + (x + dx) % nx for dz, dx in order}
-    across = [(sec + d) % sections for d in range(1, sections)]
-    barrier = pltpu.get_barrier_semaphore()
-    for o in order:
-        pl.semaphore_signal(barrier, inc=1, device_id=(sec, peer_of[o]), device_id_type=MESH)
-    for peer in across:
-        pl.semaphore_signal(barrier, inc=1, device_id=(peer, rep), device_id_type=MESH)
 
     ids_copy.wait()
     lane = lax.broadcasted_iota(jnp.int32, (1, LANES), 1)
@@ -84,8 +77,8 @@
             both_rows = both_rows + jnp.where(slot_of == s, target, 0)
         else:
             both_rows = both_rows + jnp.where(slot_of == s - DIRECT, target * base, 0)
-    rows_out[...] = both_rows
-    rows_in[pl.ds(rep, 1)] = both_rows
+    rows_out[0:1] = both_rows
+    rows_x[pl.ds(x, 1)] = both_rows
 
     for c in range(chunks):
         for copy in loads[c]:
@@ -93,8 +86,7 @@
         for b in range(c * step, (c + 1) * step):
             res[b] = grad[b].astype(f32) + res[b]
 
-    shift = nz // 2 + 1
-    far_steps = 3
+    half = nz // 2
     for pair in range(DIRECT // 2, slots // 2):
         picked = []
         for h in range(2):
@@ -105,7 +97,7 @@
         both = jnp.concatenate(picked, axis=0).astype(bf16)
         rows = slice((pair - DIRECT // 2) * 2 * BLK, (pair - DIRECT // 2 + 1) * 2 * BLK)
         for zd in range(nz):
-            place = (zd - z + shift + nz) % nz
+            place = (zd // half + z // half + 1) % 2 * half + zd % half
             for xd in range(nx):
                 r = zd * nx + xd
                 packed_ext[xd, pl.ds(place, 1), rows, :] = both[None, :, r * cols : (r + 1) * cols]
@@ -114,68 +106,94 @@
         rows = slice(pair * 2 * BLK, (pair + 1) * 2 * BLK)
         for r in range(replicas):
             packed[r, rows, :] = both[:, r * cols : (r + 1) * cols]
-    recv[pl.ds(rep, 1)] = packed[pl.ds(rep, 1)]
+    recv[pl.ds((half + z % half) * nx + x, 1)] = packed[pl.ds(rep, 1)]
     recv_ext[pl.ds(x, 1)] = packed_ext[pl.ds(x, 1)]
 
-    pl.semaphore_wait(barrier, len(order) + len(across))
-
-    halves = (pl.ds(0, far_steps), pl.ds(far_steps, nz - far_steps))
-    for h in range(2):
+    pl.semaphore_wait(barrier, len(column) + len(line) + len(across))
+    for dx in (2, 1, 3):
+        pl.semaphore_signal(column_in.at[x], inc=1, device_id=(sec, line[dx]), device_id_type=MESH)
+
+    halves = (pl.ds(0, half), pl.ds(half, half))
+    for dx in sorted(range(1, nx), key=lambda d: -ring_far(d, nx)):
+        pltpu.make_async_remote_copy(
+            rows_out.at[pl.ds(0, 1)], rows_x.at[pl.ds(x, 1)], rows_x_send, rows_x_recv,
+            device_id=(sec, z * nx + (x + dx) % nx), device_id_type=MESH,
+        ).start()
+    def send_ext(h):
         for dx in sorted(range(1, nx), key=lambda d: -ring_far(d, nx)):
             xd = (x + dx) % nx
             pltpu.make_async_remote_copy(
                 packed_ext.at[xd, halves[h]], recv_ext.at[x, halves[h]], ext_send.at[h], ext_recv.at[h],
                 device_id=(sec, z * nx + xd), device_id_type=MESH,
             ).start()
-    for o in order:
-        pltpu.make_async_remote_copy(
-            rows_out, rows_in.at[pl.ds(rep, 1)], rows_send, rows_recv, device_id=(sec, peer_of[o]), device_id_type=MESH
-        ).start()
-
-    def send_to(zt, dx):
+
+    def send_to(zt, dx, same):
         to = zt * nx + (x + dx) % nx
         pltpu.make_async_remote_copy(
-            packed.at[to], recv.at[rep], data_send, data_recv, device_id=(sec, to), device_id_type=MESH
+            packed.at[to], recv.at[(same * half + z % half) * nx + x], data_send, data_recv.at[same],
+            device_id=(sec, to), device_id_type=MESH,
         ).start()
 
-    half = nz // 2
     mine_half, other_half = (z // half) * half, (1 - z // half) * half
     cross = [other_half + (z + k) % half for k in (2, 1, 3, 0)]
     inner = [mine_half + (z + k) % half for k in (2, 1, 3)]
 
-    def send_cross():
-        for dx in (2, 1, 3, 0):
+    def send_cross(steps):
+        for dx in steps:
             for zt in cross:
-                send_to(zt, dx)
-
-    def send_inner():
-        for dx in (2, 1, 3, 0):
+                send_to(zt, dx, 0)
+
+    def send_inner(steps):
+        for dx in steps:
             for zt in inner:
-                send_to(zt, dx)
-        for dx in (2, 1, 3):
-            send_to(z, dx)
+                send_to(zt, dx, 1)
+            if dx:
+                send_to(z, dx, 1)
+
+    def forward_rows():
+        every = rows_x.at[pl.ds(0, nx - 1)]
+        pltpu.make_async_copy(every, every, rows_x_recv).wait()
+        quad = rows_x[...].sum(axis=0, keepdims=True)
+        rows_out[1:2] = quad
+        rows_in[pl.ds(half + z % half, 1)] = quad
+        for same, places in enumerate((cross, inner)):
+            for zt in places:
+                pltpu.make_async_remote_copy(
+                    rows_out.at[pl.ds(1, 1)], rows_in.at[pl.ds(same * half + z % half, 1)], rows_send, rows_recv,
+                    device_id=(sec, zt * nx + x), device_id_type=MESH,
+                ).start()
 
     def forward(h):
-        places = range(far_steps) if h == 0 else range(far_steps, nz)
+        start = h * half
         every = recv_ext.at[pl.ds(0, nx - 1), halves[h]]
         pltpu.make_async_copy(every, every, ext_recv.at[h]).wait()
-        total = recv_ext[0, places[0] : places[-1] + 1]
+        total = recv_ext[0, start : start + half]
         for k in range(1, nx):
-            total = total + recv_ext[k, places[0] : places[-1] + 1]
-        merged[places[0] : places[-1] + 1] = total
-        for place in sorted(places, key=lambda p: -ring_far((p - shift) % nz, nz)):
-            dz = (place - shift) % nz
-            if dz:
-                pltpu.make_async_remote_copy(
-                    merged.at[place], recv_merged.at[z], merged_send, merged_recv,
-                    device_id=(sec, ((z + dz) % nz) * nx + x), device_id_type=MESH,
-                ).start()
-            else:
-                recv_merged[pl.ds(z, 1)] = total[place - places[0] : place - places[0] + 1]
-
-    send_cross()
+            total = total + recv_ext[k, start : start + half]
+        merged[start : start + half] = total
+        for zt in (inner if h else cross):
+            pltpu.make_async_remote_copy(
+                merged.at[start + zt % half], recv_merged.at[z], merged_send, merged_recv,
+                device_id=(sec, zt * nx + x), device_id_type=MESH,
+            ).start()
+        if h:
+            recv_merged[pl.ds(z, 1)] = merged[pl.ds(start + z % half, 1)]
+
+    def column_ready(dx):
+        pl.semaphore_wait(column_in.at[(x + dx) % nx], 1)
+
+    send_ext(0)
+    send_ext(1)
+    send_cross((0,))
+    column_ready(1)
+    send_cross((1,))
+    column_ready(3)
+    send_cross((3,))
+    forward_rows()
+    column_ready(2)
+    send_cross((2,))
     forward(0)
-    send_inner()
+    send_inner((0, 2, 1, 3))
     forward(1)
 
     for b in range(blocks):
@@ -186,28 +204,28 @@
         mine = res[b]
         new_res[b] = mine - mine.astype(bf16).astype(f32) * kept
 
-    every = rows_in.at[pl.ds(0, others)]
-    pltpu.make_async_copy(every, every, rows_recv).wait()
+    every_row = rows_in.at[pl.ds(0, nz - 1)]
+    pltpu.make_async_copy(every_row, every_row, rows_recv).wait()
     row = lax.broadcasted_iota(jnp.int32, (row_count, LANES), 0) + 1
     lists = rows_in[...]
     ext_rows = (lists // base).sum(axis=0, keepdims=True)
-    direct_rows = (lists % base).reshape(replicas // group, group, LANES).sum(axis=1)
+    direct_rows = lists % base
     hot_ext = jnp.where(row == ext_rows, 1.0, 0.0).astype(bf16)
     hots = [jnp.where(row == direct_rows[g : g + 1], 1.0, 0.0).astype(bf16) for g in range(replicas // group)]
 
-    every = recv.at[pl.ds(0, others)]
-    pltpu.make_async_copy(every, every, data_recv).wait()
+    summed = jnp.zeros((row_count, cols), f32)
+    for same in range(2):
+        every = recv.at[pl.ds(same * half * nx, half * nx - same)]
+        pltpu.make_async_copy(every, every, data_recv.at[same]).wait()
+        for g in range(same * half, (same + 1) * half):
+            held = recv[g * group : (g + 1) * group].reshape(LANES, cols)
+            summed = summed + jnp.dot(hots[g], held, preferred_element_type=f32)
     every = recv_merged.at[pl.ds(0, nz - 1)]
     pltpu.make_async_copy(every, every, merged_recv).wait()
-
     ext = recv_merged[0]
     for k in range(1, nz):
         ext = ext + recv_merged[k]
-    summed = jnp.dot(hot_ext, jnp.concatenate([ext] * group, axis=0), preferred_element_type=f32)
-    for g, hot in enumerate(hots):
-        held = recv[g * group : (g + 1) * group].reshape(LANES, cols)
-        summed = summed + jnp.dot(hot, held, preferred_element_type=f32)
-
+    summed = summed + jnp.dot(hot_ext, jnp.concatenate([ext] * group, axis=0), preferred_element_type=f32)
     summed_out[...] = summed
     device = sec * replicas + rep
     square_out[...] = (summed * summed).reshape(row_count // 8, 8, cols).sum(axis=0).sum(axis=0, keepdims=True)
@@ -232,8 +250,9 @@
     pltpu.make_async_copy(every_square, every_square, square_recv).wait()
     every = packed.at[pl.ds(0, others)]
     pltpu.make_async_copy(every, every, data_send).wait()
-    every = rows_in.at[pl.ds(0, others)]
-    pltpu.make_async_copy(every, every, rows_send).wait()
+    every = rows_x.at[pl.ds(0, nx - 1)]
+    pltpu.make_async_copy(every, every, rows_x_send).wait()
+    pltpu.make_async_copy(every_row, every_row, rows_send).wait()
     for h in range(2):
         every = recv_ext.at[pl.ds(0, nx - 1), halves[h]]
         pltpu.make_async_copy(every, every, ext_send.at[h]).wait()
@@ -347,15 +366,16 @@
             pltpu.VMEM(shape, f32),
             pltpu.VMEM((replicas, direct_rows, cols), bf16),
             pltpu.VMEM((nx, nz, ext_rows, cols), bf16),
-            pltpu.VMEM((1, LANES), i32),
+            pltpu.VMEM((2, LANES), i32),
             pltpu.VMEM((replicas, direct_rows, cols), bf16),
             pltpu.VMEM((nx, nz, ext_rows, cols), bf16),
             pltpu.VMEM((nz, ext_rows, cols), bf16),
             pltpu.VMEM((nz, ext_rows, cols), bf16),
-            pltpu.VMEM((replicas, LANES), i32),
+            pltpu.VMEM((nx, LANES), i32),
+            pltpu.VMEM((nz, LANES), i32),
             pltpu.VMEM((1, cols), f32),
             pltpu.SMEM((1, slots), i32),
-            dma, dma((2, 4)), dma, dma, dma, dma, dma((2,)), dma((2,)), dma, dma, dma, dma,
+            pltpu.SemaphoreType.REGULAR((nx,)), dma, dma((2, 4)), dma, dma((2,)), dma, dma, dma, dma, dma((2,)), dma((2,)), dma, dma, dma, dma,
         ],
         compiler_params=pltpu.CompilerParams(collective_id=0, has_side_effects=True),
     )(gradient, residual, block_ids, block_counts)

time: 32 us -> 31.5 us (0.984)
  Pallas kernels: 30.6 us -> 30 us
    pallas_call x1, Pallas kernels: 27 us -> 26.4 us  [per_device(): pl.pallas_call(functools.partial(kernel, nz, nx, sections), out_shape=(pl...]
where the time goes in v5:
time: 31.5 us; the launch traced here: 31.3 us
  Pallas kernels  30 us (95%)
  between operations  1.29 us (4%)
    pallas_call x1, Pallas kernels, per_device(): pl.pallas_call(functools.partial(kernel, nz, nx, sections), out_shape=(pl...  26.4 us
    pallas_call x1, Pallas kernels, per_device(): pl.pallas_call(functools.partial(ahead, nx), out_shape=pltpu.HBM(shape, f...  2.88 us
    pallas_call x1, Pallas kernels, per_device(): pl.pallas_call(functools.partial(finish, count_total, nx), out_shape=(plt...  0.8 us

profile of v5, /device:TPU:1, one launch (start us, length us, event | category | flops | bytes accessed | tf_op | source)
XLA Modules:
  0.0 31.3 jit_solution(11244817358453922196)
XLA Ops:
  1.3 2.9 %shard_map.60._ = f32[16,8,4096]{2,1,0:T(8,128)} custom-call(bf16[16,8,4096]{2,1,0:T(8,128)(2,1)} %bitcast.6, f32[16,8,4096]{2,1,0:T(8,128)} %bitcast.3, s32[1,8]{1,0:T(1,128)} %ids_hbm.3, s32[1,1]{1,0:T(1,128)S(6)} %copy.8.count_in.count_ref), custom_call_target="tpu_custom_call" | custom-call | tf_op jit(solution)/shard_map/pallas_call | solution.py:350
  4.2 26.4 %shard_map.59 = (f32[16,8,4096]{2,1,0:T(8,128)S(1)}, f32[128,128]{1,0:T(8,128)S(1)}, f32[256,128]{1,0:T(8,128)S(1)}) custom-call(bf16[16,8,4096]{2,1,0:T(8,128)(2,1)} %bitcast.7, f32[16,8,4096]{2,1,0:T(8,128)} %bitcast.4, s32[1,8]{1,0:T(1,128)} %ids_hbm.3, s32[1,1]{1,0:T(1,128)S(6)} %copy.8.count_in.count_ref), custom_call_target="tpu_custom_call" | custom-call | tf_op jit(solution)/shard_map/pallas_call | solution.py:357
  30.5 0.8 %shard_map.61 = (f32[16,8,4096]{2,1,0:T(8,128)}, bf16[128,128]{1,0:T(8,128)(2,1)}) custom-call(f32[16,8,4096]{2,1,0:T(8,128)S(1)} %get-tuple-element.7.new_res, f32[128,128]{1,0:T(8,128)S(1)} %get-tuple-element.8.summed, f32[256,128]{1,0:T(8,128)S(1)} %get-tuple-element.9.squares, f32[16,8,4096]{2,1,0:T(8,128)} %shard_map.60._), custom_call_target="tpu_custom_call", output_to_operand_aliasing={{0}: (3, {})} | custom-call | tf_op jit(solution)/shard_map/pallas_call | solution.py:383

commit v6 on v5

--- a/solution.py
+++ b/solution.py
@@ -189,11 +189,11 @@
     send_cross((1,))
     column_ready(3)
     send_cross((3,))
-    forward_rows()
     column_ready(2)
     send_cross((2,))
+    forward_rows()
     forward(0)
-    send_inner((0, 2, 1, 3))
+    send_inner((2, 1, 3, 0))
     forward(1)
 
     for b in range(blocks):

time: 31.5 us -> 31.1 us (0.987)
    pallas_call x1, Pallas kernels: 26.4 us -> 26 us  [per_device(): pl.pallas_call(functools.partial(kernel, nz, nx, sections), out_shape=(pl...]
where the time goes in v6:
time: 31.1 us; the launch traced here: 31 us
  Pallas kernels  29.7 us (95%)
  between operations  1.29 us (4%)
    pallas_call x1, Pallas kernels, per_device(): pl.pallas_call(functools.partial(kernel, nz, nx, sections), out_shape=(pl...  26 us
    pallas_call x1, Pallas kernels, per_device(): pl.pallas_call(functools.partial(ahead, nx), out_shape=pltpu.HBM(shape, f...  2.88 us
    pallas_call x1, Pallas kernels, per_device(): pl.pallas_call(functools.partial(finish, count_total, nx), out_shape=(plt...  0.8 us

profile of v6, /device:TPU:1, one launch (start us, length us, event | category | flops | bytes accessed | tf_op | source)
XLA Modules:
  0.0 31.0 jit_solution(5703895825008049823)
XLA Ops:
  1.3 2.9 %shard_map.60._ = f32[16,8,4096]{2,1,0:T(8,128)} custom-call(bf16[16,8,4096]{2,1,0:T(8,128)(2,1)} %bitcast.6, f32[16,8,4096]{2,1,0:T(8,128)} %bitcast.3, s32[1,8]{1,0:T(1,128)} %ids_hbm.3, s32[1,1]{1,0:T(1,128)S(6)} %copy.8.count_in.count_ref), custom_call_target="tpu_custom_call" | custom-call | tf_op jit(solution)/shard_map/pallas_call | solution.py:350
  4.2 26.0 %shard_map.59 = (f32[16,8,4096]{2,1,0:T(8,128)S(1)}, f32[128,128]{1,0:T(8,128)S(1)}, f32[256,128]{1,0:T(8,128)S(1)}) custom-call(bf16[16,8,4096]{2,1,0:T(8,128)(2,1)} %bitcast.7, f32[16,8,4096]{2,1,0:T(8,128)} %bitcast.4, s32[1,8]{1,0:T(1,128)} %ids_hbm.3, s32[1,1]{1,0:T(1,128)S(6)} %copy.8.count_in.count_ref), custom_call_target="tpu_custom_call" | custom-call | tf_op jit(solution)/shard_map/pallas_call | solution.py:357
  30.2 0.8 %shard_map.61 = (f32[16,8,4096]{2,1,0:T(8,128)}, bf16[128,128]{1,0:T(8,128)(2,1)}) custom-call(f32[16,8,4096]{2,1,0:T(8,128)S(1)} %get-tuple-element.7.new_res, f32[128,128]{1,0:T(8,128)S(1)} %get-tuple-element.8.summed, f32[256,128]{1,0:T(8,128)S(1)} %get-tuple-element.9.squares, f32[16,8,4096]{2,1,0:T(8,128)} %shard_map.60._), custom_call_target="tpu_custom_call", output_to_operand_aliasing={{0}: (3, {})} | custom-call | tf_op jit(solution)/shard_map/pallas_call | solution.py:383

commit v7 on v6

--- a/solution.py
+++ b/solution.py
@@ -191,9 +191,10 @@
     send_cross((3,))
     column_ready(2)
     send_cross((2,))
+    send_inner((0, 2))
     forward_rows()
     forward(0)
-    send_inner((2, 1, 3, 0))
+    send_inner((1, 3))
     forward(1)
 
     for b in range(blocks):

time: 31.1 us -> 30.9 us (level)
  no operation moved by 1% of the time
where the time goes in v7:
time: 30.9 us; the launch traced here: 30.8 us
  Pallas kernels  29.5 us (95%)
  between operations  1.29 us (4%)
    pallas_call x1, Pallas kernels, per_device(): pl.pallas_call(functools.partial(kernel, nz, nx, sections), out_shape=(pl...  25.8 us
    pallas_call x1, Pallas kernels, per_device(): pl.pallas_call(functools.partial(ahead, nx), out_shape=pltpu.HBM(shape, f...  2.88 us
    pallas_call x1, Pallas kernels, per_device(): pl.pallas_call(functools.partial(finish, count_total, nx), out_shape=(plt...  0.8 us

profile of v7, /device:TPU:1, one launch (start us, length us, event | category | flops | bytes accessed | tf_op | source)
XLA Modules:
  0.0 30.8 jit_solution(11316099299475001507)
XLA Ops:
  1.3 2.9 %shard_map.60._ = f32[16,8,4096]{2,1,0:T(8,128)} custom-call(bf16[16,8,4096]{2,1,0:T(8,128)(2,1)} %bitcast.6, f32[16,8,4096]{2,1,0:T(8,128)} %bitcast.3, s32[1,8]{1,0:T(1,128)} %ids_hbm.3, s32[1,1]{1,0:T(1,128)S(6)} %copy.8.count_in.count_ref), custom_call_target="tpu_custom_call" | custom-call | tf_op jit(solution)/shard_map/pallas_call | solution.py:351
  4.2 25.8 %shard_map.59 = (f32[16,8,4096]{2,1,0:T(8,128)S(1)}, f32[128,128]{1,0:T(8,128)S(1)}, f32[256,128]{1,0:T(8,128)S(1)}) custom-call(bf16[16,8,4096]{2,1,0:T(8,128)(2,1)} %bitcast.7, f32[16,8,4096]{2,1,0:T(8,128)} %bitcast.4, s32[1,8]{1,0:T(1,128)} %ids_hbm.3, s32[1,1]{1,0:T(1,128)S(6)} %copy.8.count_in.count_ref), custom_call_target="tpu_custom_call" | custom-call | tf_op jit(solution)/shard_map/pallas_call | solution.py:358
  30.0 0.8 %shard_map.61 = (f32[16,8,4096]{2,1,0:T(8,128)}, bf16[128,128]{1,0:T(8,128)(2,1)}) custom-call(f32[16,8,4096]{2,1,0:T(8,128)S(1)} %get-tuple-element.7.new_res, f32[128,128]{1,0:T(8,128)S(1)} %get-tuple-element.8.summed, f32[256,128]{1,0:T(8,128)S(1)} %get-tuple-element.9.squares, f32[16,8,4096]{2,1,0:T(8,128)} %shard_map.60._), custom_call_target="tpu_custom_call", output_to_operand_aliasing={{0}: (3, {})} | custom-call | tf_op jit(solution)/shard_map/pallas_call | solution.py:384

commit v8 on v7

--- a/solution.py
+++ b/solution.py
@@ -185,13 +185,14 @@
     send_ext(0)
     send_ext(1)
     send_cross((0,))
+    send_inner((0,))
     column_ready(1)
     send_cross((1,))
     column_ready(3)
     send_cross((3,))
     column_ready(2)
     send_cross((2,))
-    send_inner((0, 2))
+    send_inner((2,))
     forward_rows()
     forward(0)
     send_inner((1, 3))

time: 30.9 us -> 30.9 us (level)
  no operation moved by 1% of the time
where the time goes in v8:
time: 30.9 us; the launch traced here: 30.8 us
  Pallas kernels  29.5 us (95%)
  between operations  1.29 us (4%)
    pallas_call x1, Pallas kernels, per_device(): pl.pallas_call(functools.partial(kernel, nz, nx, sections), out_shape=(pl...  25.8 us
    pallas_call x1, Pallas kernels, per_device(): pl.pallas_call(functools.partial(ahead, nx), out_shape=pltpu.HBM(shape, f...  2.88 us
    pallas_call x1, Pallas kernels, per_device(): pl.pallas_call(functools.partial(finish, count_total, nx), out_shape=(plt...  0.8 us

profile of v8, /device:TPU:1, one launch (start us, length us, event | category | flops | bytes accessed | tf_op | source)
XLA Modules:
  0.0 30.8 jit_solution(3264726009858782095)
XLA Ops:
  1.3 2.9 %shard_map.60._ = f32[16,8,4096]{2,1,0:T(8,128)} custom-call(bf16[16,8,4096]{2,1,0:T(8,128)(2,1)} %bitcast.6, f32[16,8,4096]{2,1,0:T(8,128)} %bitcast.3, s32[1,8]{1,0:T(1,128)} %ids_hbm.3, s32[1,1]{1,0:T(1,128)S(6)} %copy.8.count_in.count_ref), custom_call_target="tpu_custom_call" | custom-call | tf_op jit(solution)/shard_map/pallas_call | solution.py:352
  4.2 25.8 %shard_map.59 = (f32[16,8,4096]{2,1,0:T(8,128)S(1)}, f32[128,128]{1,0:T(8,128)S(1)}, f32[256,128]{1,0:T(8,128)S(1)}) custom-call(bf16[16,8,4096]{2,1,0:T(8,128)(2,1)} %bitcast.7, f32[16,8,4096]{2,1,0:T(8,128)} %bitcast.4, s32[1,8]{1,0:T(1,128)} %ids_hbm.3, s32[1,1]{1,0:T(1,128)S(6)} %copy.8.count_in.count_ref), custom_call_target="tpu_custom_call" | custom-call | tf_op jit(solution)/shard_map/pallas_call | solution.py:359
  30.0 0.8 %shard_map.61 = (f32[16,8,4096]{2,1,0:T(8,128)}, bf16[128,128]{1,0:T(8,128)(2,1)}) custom-call(f32[16,8,4096]{2,1,0:T(8,128)S(1)} %get-tuple-element.7.new_res, f32[128,128]{1,0:T(8,128)S(1)} %get-tuple-element.8.summed, f32[256,128]{1,0:T(8,128)S(1)} %get-tuple-element.9.squares, f32[16,8,4096]{2,1,0:T(8,128)} %shard_map.60._), custom_call_target="tpu_custom_call", output_to_operand_aliasing={{0}: (3, {})} | custom-call | tf_op jit(solution)/shard_map/pallas_call | solution.py:385
